TPU v7x, 256 devices: a whole 4x4x8 slice. The times are simulated.
256 devices in a mesh: chain: 256 (over y, x, z, core).
Axes of the slice: x: 4, y: 4, z: 8, core: 2. Of those that a mesh axis runs over, the one named last changes fastest.
Arguments:
- right_side: float32 [8, 32768], P(None, 'chain'), may hold values from -6 to 6
- diag_block: float32 [8, 8, 32768], P(None, None, 'chain'), may hold values from -2 to 2
- below_block: float32 [8, 8, 32768], P(None, None, 'chain'), may hold values from -2 to 2
- above_block: float32 [8, 8, 32768], P(None, None, 'chain'), may hold values from -2 to 2
- lower_level: float32 [15, 8, 8, 32768], P(None, None, None, 'chain'), may hold values from -0.5 to 0.5
- upper_level: float32 [15, 8, 8, 32768], P(None, None, None, 'chain'), may hold values from -0.5 to 0.5
- final_block: float32 [8, 8, 32768], P(None, None, 'chain'), may hold values from -1 to 1
Outputs:
- basis: float32 [4, 8, 32768], P(None, None, 'chain')
- hess: float32 [4, 3], replicated
All inputs are finite; a program needn't handle non-finite values.
Results may differ from a plain program's by a relative error of at most 0.0001.
Values sent between devices are 32-bit elements; how exact they have to be, the bound alone decides.
A program may use at most 64 MiB of HBM per device.

v0:
```python
import functools

import jax
import jax.numpy as jnp
from jax import lax
from jax.sharding import Mesh
from jax.sharding import PartitionSpec as P

ITERS = 3
CHAIN = ("chain_0", "chain_1", "chain_2", "chain_3")


EPS = 1e-06


def padded_2(x, sides, width):
    for axis, dim in sides:
        peers, length = (lax.axis_size(axis), x.shape[dim])
        up = [(i, (i + 1) % peers) for i in range(peers - 1)]
        down = [(j, i) for i, j in up]
        last = lax.slice_in_dim(x, length - width, length, axis=dim)
        initial = lax.slice_in_dim(x, 0, width, axis=dim)
        before = lax.ppermute(last, axis, up)
        after = lax.ppermute(initial, axis, down)
        x = jnp.concatenate([before, x, after], axis=dim)
    return x


def from_behind(x, axis, by):
    peers = lax.axis_size(axis)
    pairs = [(i, i + by) for i in range(peers) if 0 <= i + by < peers]
    return lax.ppermute(x, axis, pairs)


def one_axis_at_a_time(x, axes):
    return functools.reduce(lax.psum, axes, x)


def blockmul(blocks, field):
    return jnp.einsum("abi,bi->ai", blocks, field, precision=lax.Precision.HIGHEST)


def on_device(
    right_side, diag_block, below_block, above_block, lower_level, upper_level, final_block
):
    rows_here = right_side.shape[1]
    devices = lax.axis_size(CHAIN)
    whole = rows_here * devices
    count = right_side.shape[0] * whole
    depth = lower_level.shape[0]
    near = [level for level in range(depth) if 2**level < rows_here]
    far = [level for level in range(depth) if 2**level >= rows_here and 2**level < whole]
    reach = sum((2**level for level in near))
    stacked_coef = jnp.concatenate([lower_level[: len(near)], upper_level[: len(near)]], 0)
    wide_coef = padded_2(stacked_coef, ((CHAIN, 3),), reach)
    start_sum = one_axis_at_a_time(jnp.sum(right_side * right_side), CHAIN)
    basis = [right_side / jnp.sqrt(start_sum / count + EPS)]
    hess = jnp.zeros((ITERS + 1, ITERS), jnp.float32)
    for column in range(ITERS):
        precondition_field = basis[column]
        current = padded_2(precondition_field, ((CHAIN, 1),), reach)
        offset = 0
        for position in range(len(near)):
            stride = 2 ** near[position]
            length = current.shape[1]
            first_col = offset + stride
            last_col = offset + length - stride
            low_coef = wide_coef[position][:, :, first_col:last_col]
            high_coef = wide_coef[len(near) + position][:, :, first_col:last_col]
            current = (
                current[:, stride : length - stride]
                + blockmul(low_coef, current[:, : length - 2 * stride])
                + blockmul(high_coef, current[:, 2 * stride :])
            )
            offset = first_col
        precondition_field = current
        for precondition_level in far:
            hops = 2**precondition_level // rows_here
            below_rows = from_behind(precondition_field, CHAIN, hops)
            above_rows = from_behind(precondition_field, CHAIN, -hops)
            precondition_field = (
                precondition_field
                + blockmul(lower_level[precondition_level], below_rows)
                + blockmul(upper_level[precondition_level], above_rows)
            )
        field = precondition_field + blockmul(final_block, precondition_field)
        padded = padded_2(field, ((CHAIN, 1),), 1)
        result = 2.0 * field + blockmul(diag_block, field)
        result = result + blockmul(below_block, padded[:, :rows_here])
        vector = result + blockmul(above_block, padded[:, 2:])
        stacked = jnp.stack(basis)
        local_dots = jnp.einsum("kai,ai->k", stacked, vector, precision=lax.Precision.HIGHEST)
        dot_sums, square_sum = (
            one_axis_at_a_time(local_dots, CHAIN),
            one_axis_at_a_time(jnp.sum(vector * vector), CHAIN),
        )
        dots = dot_sums / count
        vector = vector - jnp.einsum("k,kai->ai", dots, stacked, precision=lax.Precision.HIGHEST)
        squares = square_sum / count - jnp.sum(dots * dots)
        length = jnp.sqrt(squares + EPS)
        basis.append(vector / length)
        hess = hess.at[: column + 1, column].set(dots).at[column + 1, column].set(length)
    return (jnp.stack(basis), hess)


def solution(mesh):
    finer = Mesh(mesh.devices.reshape(4, 4, 8, 2), ("chain_0", "chain_1", "chain_2", "chain_3"))
    in_specs = (
        P(None, CHAIN),
        P(None, None, CHAIN),
        P(None, None, CHAIN),
        P(None, None, CHAIN),
        P(None, None, None, CHAIN),
        P(None, None, None, CHAIN),
        P(None, None, CHAIN),
    )
    out_specs = (P(None, None, CHAIN), P())
    return jax.shard_map(
        on_device, mesh=finer, in_specs=in_specs, out_specs=out_specs, check_vma=False
    )
```

profile of v0, /device:TPU:1, one launch (start us, length us, event | category | flops | bytes accessed | tf_op | source)
XLA Modules:
  0.0 551.1 jit_solution(3675210418324190210)
XLA Ops:
  3.0 10.2 %psum.196 = f32[]{:T(128)} all-reduce(f32[]{:T(128)} %multiply_reduce_fusion.58), channel_id=1, replica_groups=mesh['chain_0'=4,'chain_1'=4,'chain_2'=8,'chain_3'=2] {'chain_0'}, use_global_device_ids=true, to_apply=%region_1.0 | all-reduce | flops 1 | bytes 8 | tf_op jit(solution)/shard_map/psum | solution.py:36
  14.1 9.4 %psum.197 = f32[]{:T(128)} all-reduce(f32[]{:T(128)} %psum.196), channel_id=1, replica_groups=mesh['chain_0'=4,'chain_1'=4,'chain_2'=8,'chain_3'=2] {'chain_1'}, use_global_device_ids=true, to_apply=%region_2.0 | all-reduce | flops 1 | bytes 8 | tf_op jit(solution)/shard_map/psum | solution.py:36
  23.7 7.8 %collective-permute-start.2 = (f32[14,8,8,127]{3,2,1,0:T(8,128)S(1)}, f32[14,8,8,127]{3,2,1,0:T(8,128)S(1)}, u32[]{:S(2)}, u32[]{:S(2)}) collective-permute-start(f32[14,8,8,127]{3,2,1,0:T(8,128)S(1)} %get-tuple-element.121), channel_id=1, source_target_pairs={{0,1},{1,2},{2,3},{3,4},{4,5},{5,6},{6,7},{7,8},{8,9},{9,10},{10,1... | collective-permute-start | bytes 1365512 | tf_op jit(solution)/shard_map/ppermute | solution.py:23
  31.5 17.9 %psum.198 = f32[]{:T(128)} all-reduce(f32[]{:T(128)} %psum.197), channel_id=1, replica_groups=mesh['chain_0'=4,'chain_1'=4,'chain_2'=8,'chain_3'=2] {'chain_2'}, use_global_device_ids=true, to_apply=%region_3.0 | all-reduce | flops 1 | bytes 8 | tf_op jit(solution)/shard_map/psum | solution.py:36
  49.4 3.2 collective-permute-start.3
  52.6 3.1 psum.199
  69.0 3.6 collective-permute-start.4
  75.5 4.0 collective-permute-start.6
  82.4 6.6 %collective-permute-start.8 = (f32[8,128]{1,0:T(8,128)S(1)}, f32[8,128]{1,0:T(8,128)S(1)}, u32[]{:S(2)}, u32[]{:S(2)}) collective-permute-start(f32[8,128]{1,0:T(8,128)S(1)} %bitcast_add_fusion.56), channel_id=1, source_target_pairs={{0,4},{1,5},{2,6},{3,7},{4,8},{5,9},{6,10},{7,11},{8,12},{9,13},{1... | collective-permute-start | bytes 12296 | tf_op jit(solution)/shard_map/ppermute | solution.py:32
  91.9 11.2 %collective-permute-start.10 = (f32[8,128]{1,0:T(8,128)S(1)}, f32[8,128]{1,0:T(8,128)S(1)}, u32[]{:S(2)}, u32[]{:S(2)}) collective-permute-start(f32[8,128]{1,0:T(8,128)S(1)} %bitcast_add_fusion.54), channel_id=1, source_target_pairs={{0,8},{1,9},{2,10},{3,11},{4,12},{5,13},{6,14},{7,15},{8,16},{9,17... | collective-permute-start | bytes 12296 | tf_op jit(solution)/shard_map/ppermute | solution.py:32
  106.0 11.4 %collective-permute-start.12 = (f32[8,128]{1,0:T(8,128)S(1)}, f32[8,128]{1,0:T(8,128)S(1)}, u32[]{:S(2)}, u32[]{:S(2)}) collective-permute-start(f32[8,128]{1,0:T(8,128)S(1)} %bitcast_add_fusion.52), channel_id=1, source_target_pairs={{0,16},{1,17},{2,18},{3,19},{4,20},{5,21},{6,22},{7,23},{8,24},{9,... | collective-permute-start | bytes 12296 | tf_op jit(solution)/shard_map/ppermute | solution.py:32
  120.2 6.8 %collective-permute-start.14 = (f32[8,128]{1,0:T(8,128)S(1)}, f32[8,128]{1,0:T(8,128)S(1)}, u32[]{:S(2)}, u32[]{:S(2)}) collective-permute-start(f32[8,128]{1,0:T(8,128)S(1)} %bitcast_add_fusion.50), channel_id=1, source_target_pairs={{0,32},{1,33},{2,34},{3,35},{4,36},{5,37},{6,38},{7,39},{8,40},{9,... | collective-permute-start | bytes 12296 | tf_op jit(solution)/shard_map/ppermute | solution.py:32
  130.0 17.8 %collective-permute-start.16 = (f32[8,128]{1,0:T(8,128)S(1)}, f32[8,128]{1,0:T(8,128)S(1)}, u32[]{:S(2)}, u32[]{:S(2)}) collective-permute-start(f32[8,128]{1,0:T(8,128)S(1)} %bitcast_add_fusion.48), channel_id=1, source_target_pairs={{0,64},{1,65},{2,66},{3,67},{4,68},{5,69},{6,70},{7,71},{8,72},{9,... | collective-permute-start | bytes 12296 | tf_op jit(solution)/shard_map/ppermute | solution.py:32
  150.7 5.5 collective-permute-start.18
  157.9 11.4 %collective-permute-start.20 = (f32[8,1]{1,0:T(8,128)S(1)}, f32[8,1]{1,0:T(8,128)S(1)}, u32[]{:S(2)}, u32[]{:S(2)}) collective-permute-start(f32[8,1]{1,0:T(8,128)S(1)} %get-tuple-element.179), channel_id=1, source_target_pairs={{0,1},{1,2},{2,3},{3,4},{4,5},{5,6},{6,7},{7,8},{8,9},{9,10},{10,1... | collective-permute-start | bytes 104 | tf_op jit(solution)/shard_map/ppermute | solution.py:23
  175.0 11.6 %all-reduce.9 = (f32[]{:T(128)}, f32[1]{0:T(128)}) all-reduce(f32[]{:T(128)} %get-tuple-element.77, f32[1]{0:T(128)} %bitcast.285), channel_id=1, replica_groups=mesh['chain_0'=4,'chain_1'=4,'chain_2'=8,'chain_3'=2] {'chain_0'}, use_global_device_ids=true, to_apply=%region_10.0 | all-reduce | flops 2 | bytes 16 | tf_op jit(solution)/shard_map/psum | solution.py:36
  186.6 7.7 %all-reduce.6 = (f32[]{:T(128)}, f32[1]{0:T(128)}) all-reduce(f32[]{:T(128)} %get-tuple-element.94, f32[1]{0:T(128)} %get-tuple-element.95), channel_id=1, replica_groups=mesh['chain_0'=4,'chain_1'=4,'chain_2'=8,'chain_3'=2] {'chain_1'}, use_global_device_ids=true, to_apply=%region_11.0 | all-reduce | flops 2 | bytes 16 | tf_op jit(solution)/shard_map/psum | solution.py:36
  194.3 16.9 %all-reduce.3 = (f32[]{:T(128)}, f32[1]{0:T(128)}) all-reduce(f32[]{:T(128)} %get-tuple-element.88, f32[1]{0:T(128)} %get-tuple-element.89), channel_id=1, replica_groups=mesh['chain_0'=4,'chain_1'=4,'chain_2'=8,'chain_3'=2] {'chain_2'}, use_global_device_ids=true, to_apply=%region_12.0 | all-reduce | flops 2 | bytes 16 | tf_op jit(solution)/shard_map/psum | solution.py:36
  211.2 6.5 %all-reduce.12 = (f32[]{:T(128)}, f32[1]{0:T(128)}) all-reduce(f32[]{:T(128)} %get-tuple-element.82, f32[1]{0:T(128)} %get-tuple-element.83), channel_id=1, replica_groups=mesh['chain_0'=4,'chain_1'=4,'chain_2'=8,'chain_3'=2] {'chain_3'}, use_global_device_ids=true, to_apply=%region_13.0 | all-reduce | flops 2 | bytes 16 | tf_op jit(solution)/shard_map/psum | solution.py:36
  220.4 4.0 collective-permute-start.22
  233.8 3.6 collective-permute-start.24
  240.3 4.0 collective-permute-start.26
  247.2 4.9 collective-permute-start.28
  255.0 11.2 %collective-permute-start.30 = (f32[8,128]{1,0:T(8,128)S(1)}, f32[8,128]{1,0:T(8,128)S(1)}, u32[]{:S(2)}, u32[]{:S(2)}) collective-permute-start(f32[8,128]{1,0:T(8,128)S(1)} %bitcast_add_fusion.34), channel_id=1, source_target_pairs={{0,8},{1,9},{2,10},{3,11},{4,12},{5,13},{6,14},{7,15},{8,16},{9,17... | collective-permute-start | bytes 12296 | tf_op jit(solution)/shard_map/ppermute | solution.py:32
  269.1 12.7 %collective-permute-start.32 = (f32[8,128]{1,0:T(8,128)S(1)}, f32[8,128]{1,0:T(8,128)S(1)}, u32[]{:S(2)}, u32[]{:S(2)}) collective-permute-start(f32[8,128]{1,0:T(8,128)S(1)} %bitcast_add_fusion.32), channel_id=1, source_target_pairs={{0,16},{1,17},{2,18},{3,19},{4,20},{5,21},{6,22},{7,23},{8,24},{9,... | collective-permute-start | bytes 12296 | tf_op jit(solution)/shard_map/ppermute | solution.py:32
  284.6 6.8 %collective-permute-start.34 = (f32[8,128]{1,0:T(8,128)S(1)}, f32[8,128]{1,0:T(8,128)S(1)}, u32[]{:S(2)}, u32[]{:S(2)}) collective-permute-start(f32[8,128]{1,0:T(8,128)S(1)} %bitcast_add_fusion.30), channel_id=1, source_target_pairs={{0,32},{1,33},{2,34},{3,35},{4,36},{5,37},{6,38},{7,39},{8,40},{9,... | collective-permute-start | bytes 12296 | tf_op jit(solution)/shard_map/ppermute | solution.py:32
  293.1 15.7 %collective-permute-start.36 = (f32[8,128]{1,0:T(8,128)S(1)}, f32[8,128]{1,0:T(8,128)S(1)}, u32[]{:S(2)}, u32[]{:S(2)}) collective-permute-start(f32[8,128]{1,0:T(8,128)S(1)} %bitcast_add_fusion.28), channel_id=1, source_target_pairs={{0,64},{1,65},{2,66},{3,67},{4,68},{5,69},{6,70},{7,71},{8,72},{9,... | collective-permute-start | bytes 12296 | tf_op jit(solution)/shard_map/ppermute | solution.py:32
  314.5 5.5 collective-permute-start.38
  320.8 11.9 %collective-permute-start.40 = (f32[8,1]{1,0:T(8,128)S(1)}, f32[8,1]{1,0:T(8,128)S(1)}, u32[]{:S(2)}, u32[]{:S(2)}) collective-permute-start(f32[8,1]{1,0:T(8,128)S(1)} %get-tuple-element.173), channel_id=1, source_target_pairs={{0,1},{1,2},{2,3},{3,4},{4,5},{5,6},{6,7},{7,8},{8,9},{9,10},{10,1... | collective-permute-start | bytes 104 | tf_op jit(solution)/shard_map/ppermute | solution.py:23
  338.5 11.1 %all-reduce.8 = (f32[2]{0:T(128)S(1)}, f32[]{:T(128)}) all-reduce(f32[2]{0:T(128)S(1)} %convolution_bitcast_fusion.1, f32[]{:T(128)} %get-tuple-element.104), channel_id=1, replica_groups=mesh['chain_0'=4,'chain_1'=4,'chain_2'=8,'chain_3'=2] {'chain_0'}, use_global_device_ids=true, to_apply=%region_14.0 | all-reduce | flops 3 | bytes 24 | tf_op jit(solution)/shard_map/psum | solution.py:36
  349.6 7.5 %all-reduce.5 = (f32[2]{0:T(128)S(1)}, f32[]{:T(128)}) all-reduce(f32[2]{0:T(128)S(1)} %get-tuple-element.92, f32[]{:T(128)} %get-tuple-element.93), channel_id=1, replica_groups=mesh['chain_0'=4,'chain_1'=4,'chain_2'=8,'chain_3'=2] {'chain_1'}, use_global_device_ids=true, to_apply=%region_15.0 | all-reduce | flops 3 | bytes 24 | tf_op jit(solution)/shard_map/psum | solution.py:36
  357.0 17.4 %all-reduce.2 = (f32[2]{0:T(128)S(1)}, f32[]{:T(128)}) all-reduce(f32[2]{0:T(128)S(1)} %get-tuple-element.86, f32[]{:T(128)} %get-tuple-element.87), channel_id=1, replica_groups=mesh['chain_0'=4,'chain_1'=4,'chain_2'=8,'chain_3'=2] {'chain_2'}, use_global_device_ids=true, to_apply=%region_16.0 | all-reduce | flops 3 | bytes 24 | tf_op jit(solution)/shard_map/psum | solution.py:36
  374.4 6.2 %all-reduce.11 = (f32[2]{0:T(128)S(1)}, f32[]{:T(128)}) all-reduce(f32[2]{0:T(128)S(1)} %get-tuple-element.80, f32[]{:T(128)} %get-tuple-element.81), channel_id=1, replica_groups=mesh['chain_0'=4,'chain_1'=4,'chain_2'=8,'chain_3'=2] {'chain_3'}, use_global_device_ids=true, to_apply=%region_17.0 | all-reduce | flops 3 | bytes 24 | tf_op jit(solution)/shard_map/psum | solution.py:36
  382.9 3.9 collective-permute-start.42
  396.1 3.6 collective-permute-start.44
  401.8 4.0 collective-permute-start.46
  408.5 4.9 collective-permute-start.48
  416.1 11.1 %collective-permute-start.50 = (f32[8,128]{1,0:T(8,128)S(1)}, f32[8,128]{1,0:T(8,128)S(1)}, u32[]{:S(2)}, u32[]{:S(2)}) collective-permute-start(f32[8,128]{1,0:T(8,128)S(1)} %bitcast_add_fusion.14), channel_id=1, source_target_pairs={{0,8},{1,9},{2,10},{3,11},{4,12},{5,13},{6,14},{7,15},{8,16},{9,17... | collective-permute-start | bytes 12296 | tf_op jit(solution)/shard_map/ppermute | solution.py:32
  429.3 12.9 %collective-permute-start.52 = (f32[8,128]{1,0:T(8,128)S(1)}, f32[8,128]{1,0:T(8,128)S(1)}, u32[]{:S(2)}, u32[]{:S(2)}) collective-permute-start(f32[8,128]{1,0:T(8,128)S(1)} %bitcast_add_fusion.12), channel_id=1, source_target_pairs={{0,16},{1,17},{2,18},{3,19},{4,20},{5,21},{6,22},{7,23},{8,24},{9,... | collective-permute-start | bytes 12296 | tf_op jit(solution)/shard_map/ppermute | solution.py:32
  445.7 6.9 %collective-permute-start.54 = (f32[8,128]{1,0:T(8,128)S(1)}, f32[8,128]{1,0:T(8,128)S(1)}, u32[]{:S(2)}, u32[]{:S(2)}) collective-permute-start(f32[8,128]{1,0:T(8,128)S(1)} %bitcast_add_fusion.10), channel_id=1, source_target_pairs={{0,32},{1,33},{2,34},{3,35},{4,36},{5,37},{6,38},{7,39},{8,40},{9,... | collective-permute-start | bytes 12296 | tf_op jit(solution)/shard_map/ppermute | solution.py:32
  453.3 15.7 %collective-permute-start.56 = (f32[8,128]{1,0:T(8,128)S(1)}, f32[8,128]{1,0:T(8,128)S(1)}, u32[]{:S(2)}, u32[]{:S(2)}) collective-permute-start(f32[8,128]{1,0:T(8,128)S(1)} %bitcast_add_fusion.8), channel_id=1, source_target_pairs={{0,64},{1,65},{2,66},{3,67},{4,68},{5,69},{6,70},{7,71},{8,72},{9,... | collective-permute-start | bytes 12296 | tf_op jit(solution)/shard_map/ppermute | solution.py:32
  472.2 3.0 collective-permute-done.57
  478.1 5.5 collective-permute-start.58
  484.5 11.9 %collective-permute-start.60 = (f32[8,1]{1,0:T(8,128)S(1)}, f32[8,1]{1,0:T(8,128)S(1)}, u32[]{:S(2)}, u32[]{:S(2)}) collective-permute-start(f32[8,1]{1,0:T(8,128)S(1)} %get-tuple-element.167), channel_id=1, source_target_pairs={{0,1},{1,2},{2,3},{3,4},{4,5},{5,6},{6,7},{7,8},{8,9},{9,10},{10,1... | collective-permute-start | bytes 104 | tf_op jit(solution)/shard_map/ppermute | solution.py:23
  502.2 11.0 %all-reduce.7 = (f32[3]{0:T(128)S(1)}, f32[]{:T(128)}) all-reduce(f32[3]{0:T(128)S(1)} %convolution_bitcast_fusion, f32[]{:T(128)} %get-tuple-element.102), channel_id=1, replica_groups=mesh['chain_0'=4,'chain_1'=4,'chain_2'=8,'chain_3'=2] {'chain_0'}, use_global_device_ids=true, to_apply=%region_24.0 | all-reduce | flops 4 | bytes 32 | tf_op jit(solution)/shard_map/psum | solution.py:36
  513.2 7.5 %all-reduce.4 = (f32[3]{0:T(128)S(1)}, f32[]{:T(128)}) all-reduce(f32[3]{0:T(128)S(1)} %get-tuple-element.90, f32[]{:T(128)} %get-tuple-element.91), channel_id=1, replica_groups=mesh['chain_0'=4,'chain_1'=4,'chain_2'=8,'chain_3'=2] {'chain_1'}, use_global_device_ids=true, to_apply=%region_25.0 | all-reduce | flops 4 | bytes 32 | tf_op jit(solution)/shard_map/psum | solution.py:36
  520.7 17.3 %all-reduce.1 = (f32[3]{0:T(128)S(1)}, f32[]{:T(128)}) all-reduce(f32[3]{0:T(128)S(1)} %get-tuple-element.84, f32[]{:T(128)} %get-tuple-element.85), channel_id=1, replica_groups=mesh['chain_0'=4,'chain_1'=4,'chain_2'=8,'chain_3'=2] {'chain_2'}, use_global_device_ids=true, to_apply=%region_26.0 | all-reduce | flops 4 | bytes 32 | tf_op jit(solution)/shard_map/psum | solution.py:36
  538.0 6.2 %all-reduce.10 = (f32[3]{0:T(128)S(1)}, f32[]{:T(128)}) all-reduce(f32[3]{0:T(128)S(1)} %get-tuple-element.78, f32[]{:T(128)} %get-tuple-element.79), channel_id=1, replica_groups=mesh['chain_0'=4,'chain_1'=4,'chain_2'=8,'chain_3'=2] {'chain_3'}, use_global_device_ids=true, to_apply=%region_27.0 | all-reduce | flops 4 | bytes 32 | tf_op jit(solution)/shard_map/psum | solution.py:36
  (328 shorter events, 122.2 us)
Async XLA Ops:
  23.7 40.3 %collective-permute-start.2 = (f32[14,8,8,127]{3,2,1,0:T(8,128)S(1)}, f32[14,8,8,127]{3,2,1,0:T(8,128)S(1)}, u32[]{:S(2)}, u32[]{:S(2)}) collective-permute-start(f32[14,8,8,127]{3,2,1,0:T(8,128)S(1)} %get-tuple-element.121), channel_id=1, source_target_pairs={{0,1},{1,2},{2,3},{3,4},{4,5},{5,6},{6,7},{7,8},{8,9},{9,10},{10,1... | collective-permute-start | bytes 1365512 | tf_op jit(solution)/shard_map/ppermute | solution.py:23
  49.4 14.5 %collective-permute-start.3 = (f32[14,8,8,127]{3,2,1,0:T(8,128)S(1)}, f32[14,8,8,127]{3,2,1,0:T(8,128)S(1)}, u32[]{:S(2)}, u32[]{:S(2)}) collective-permute-start(f32[14,8,8,127]{3,2,1,0:T(8,128)S(1)} %get-tuple-element.122), channel_id=1, source_target_pairs={{1,0},{2,1},{3,2},{4,3},{5,4},{6,5},{7,6},{8,7},{9,8},{10,9},{11,1... | collective-permute-start | bytes 1365512 | tf_op jit(solution)/shard_map/ppermute | solution.py:24
  58.9 4.9 collective-permute-start.1
  67.0 5.6 %collective-permute-start.5 = (f32[8,128]{1,0:T(8,128)S(1)}, f32[8,128]{1,0:T(8,128)S(1)}, u32[]{:S(2)}, u32[]{:S(2)}) collective-permute-start(f32[8,128]{1,0:T(8,128)S(1)} %fusion.80), channel_id=1, source_target_pairs={{1,0},{2,1},{3,2},{4,3},{5,4},{6,5},{7,6},{8,7},{9,8},{10,9},{11,1... | collective-permute-start | bytes 12296 | tf_op jit(solution)/shard_map/ppermute | solution.py:32
  74.2 5.3 collective-permute-start.7
  81.1 7.9 %collective-permute-start.9 = (f32[8,128]{1,0:T(8,128)S(1)}, f32[8,128]{1,0:T(8,128)S(1)}, u32[]{:S(2)}, u32[]{:S(2)}) collective-permute-start(f32[8,128]{1,0:T(8,128)S(1)} %bitcast_add_fusion.56), channel_id=1, source_target_pairs={{4,0},{5,1},{6,2},{7,3},{8,4},{9,5},{10,6},{11,7},{12,8},{13,9},{1... | collective-permute-start | bytes 12296 | tf_op jit(solution)/shard_map/ppermute | solution.py:32
  82.4 7.4 %collective-permute-start.8 = (f32[8,128]{1,0:T(8,128)S(1)}, f32[8,128]{1,0:T(8,128)S(1)}, u32[]{:S(2)}, u32[]{:S(2)}) collective-permute-start(f32[8,128]{1,0:T(8,128)S(1)} %bitcast_add_fusion.56), channel_id=1, source_target_pairs={{0,4},{1,5},{2,6},{3,7},{4,8},{5,9},{6,10},{7,11},{8,12},{9,13},{1... | collective-permute-start | bytes 12296 | tf_op jit(solution)/shard_map/ppermute | solution.py:32
  90.6 12.5 %collective-permute-start.11 = (f32[8,128]{1,0:T(8,128)S(1)}, f32[8,128]{1,0:T(8,128)S(1)}, u32[]{:S(2)}, u32[]{:S(2)}) collective-permute-start(f32[8,128]{1,0:T(8,128)S(1)} %bitcast_add_fusion.54), channel_id=1, source_target_pairs={{8,0},{9,1},{10,2},{11,3},{12,4},{13,5},{14,6},{15,7},{16,8},{17,9... | collective-permute-start | bytes 12296 | tf_op jit(solution)/shard_map/ppermute | solution.py:32
  91.9 12.0 %collective-permute-start.10 = (f32[8,128]{1,0:T(8,128)S(1)}, f32[8,128]{1,0:T(8,128)S(1)}, u32[]{:S(2)}, u32[]{:S(2)}) collective-permute-start(f32[8,128]{1,0:T(8,128)S(1)} %bitcast_add_fusion.54), channel_id=1, source_target_pairs={{0,8},{1,9},{2,10},{3,11},{4,12},{5,13},{6,14},{7,15},{8,16},{9,17... | collective-permute-start | bytes 12296 | tf_op jit(solution)/shard_map/ppermute | solution.py:32
  104.7 12.7 %collective-permute-start.13 = (f32[8,128]{1,0:T(8,128)S(1)}, f32[8,128]{1,0:T(8,128)S(1)}, u32[]{:S(2)}, u32[]{:S(2)}) collective-permute-start(f32[8,128]{1,0:T(8,128)S(1)} %bitcast_add_fusion.52), channel_id=1, source_target_pairs={{16,0},{17,1},{18,2},{19,3},{20,4},{21,5},{22,6},{23,7},{24,8},{25... | collective-permute-start | bytes 12296 | tf_op jit(solution)/shard_map/ppermute | solution.py:32
  106.0 12.2 %collective-permute-start.12 = (f32[8,128]{1,0:T(8,128)S(1)}, f32[8,128]{1,0:T(8,128)S(1)}, u32[]{:S(2)}, u32[]{:S(2)}) collective-permute-start(f32[8,128]{1,0:T(8,128)S(1)} %bitcast_add_fusion.52), channel_id=1, source_target_pairs={{0,16},{1,17},{2,18},{3,19},{4,20},{5,21},{6,22},{7,23},{8,24},{9,... | collective-permute-start | bytes 12296 | tf_op jit(solution)/shard_map/ppermute | solution.py:32
  118.9 8.2 %collective-permute-start.15 = (f32[8,128]{1,0:T(8,128)S(1)}, f32[8,128]{1,0:T(8,128)S(1)}, u32[]{:S(2)}, u32[]{:S(2)}) collective-permute-start(f32[8,128]{1,0:T(8,128)S(1)} %bitcast_add_fusion.50), channel_id=1, source_target_pairs={{32,0},{33,1},{34,2},{35,3},{36,4},{37,5},{38,6},{39,7},{40,8},{41... | collective-permute-start | bytes 12296 | tf_op jit(solution)/shard_map/ppermute | solution.py:32
  120.2 7.6 %collective-permute-start.14 = (f32[8,128]{1,0:T(8,128)S(1)}, f32[8,128]{1,0:T(8,128)S(1)}, u32[]{:S(2)}, u32[]{:S(2)}) collective-permute-start(f32[8,128]{1,0:T(8,128)S(1)} %bitcast_add_fusion.50), channel_id=1, source_target_pairs={{0,32},{1,33},{2,34},{3,35},{4,36},{5,37},{6,38},{7,39},{8,40},{9,... | collective-permute-start | bytes 12296 | tf_op jit(solution)/shard_map/ppermute | solution.py:32
  128.7 19.2 %collective-permute-start.17 = (f32[8,128]{1,0:T(8,128)S(1)}, f32[8,128]{1,0:T(8,128)S(1)}, u32[]{:S(2)}, u32[]{:S(2)}) collective-permute-start(f32[8,128]{1,0:T(8,128)S(1)} %bitcast_add_fusion.48), channel_id=1, source_target_pairs={{64,0},{65,1},{66,2},{67,3},{68,4},{69,5},{70,6},{71,7},{72,8},{73... | collective-permute-start | bytes 12296 | tf_op jit(solution)/shard_map/ppermute | solution.py:32
  130.0 18.6 %collective-permute-start.16 = (f32[8,128]{1,0:T(8,128)S(1)}, f32[8,128]{1,0:T(8,128)S(1)}, u32[]{:S(2)}, u32[]{:S(2)}) collective-permute-start(f32[8,128]{1,0:T(8,128)S(1)} %bitcast_add_fusion.48), channel_id=1, source_target_pairs={{0,64},{1,65},{2,66},{3,67},{4,68},{5,69},{6,70},{7,71},{8,72},{9,... | collective-permute-start | bytes 12296 | tf_op jit(solution)/shard_map/ppermute | solution.py:32
  149.4 6.8 %collective-permute-start.19 = (f32[8,128]{1,0:T(8,128)S(1)}, f32[8,128]{1,0:T(8,128)S(1)}, u32[]{:S(2)}, u32[]{:S(2)}) collective-permute-start(f32[8,128]{1,0:T(8,128)S(1)} %bitcast_add_fusion.46), channel_id=1, source_target_pairs={{128,0},{129,1},{130,2},{131,3},{132,4},{133,5},{134,6},{135,7},{1... | collective-permute-start | bytes 12296 | tf_op jit(solution)/shard_map/ppermute | solution.py:32
  150.7 6.3 %collective-permute-start.18 = (f32[8,128]{1,0:T(8,128)S(1)}, f32[8,128]{1,0:T(8,128)S(1)}, u32[]{:S(2)}, u32[]{:S(2)}) collective-permute-start(f32[8,128]{1,0:T(8,128)S(1)} %bitcast_add_fusion.46), channel_id=1, source_target_pairs={{0,128},{1,129},{2,130},{3,131},{4,132},{5,133},{6,134},{7,135},{8... | collective-permute-start | bytes 12296 | tf_op jit(solution)/shard_map/ppermute | solution.py:32
  157.9 13.3 %collective-permute-start.20 = (f32[8,1]{1,0:T(8,128)S(1)}, f32[8,1]{1,0:T(8,128)S(1)}, u32[]{:S(2)}, u32[]{:S(2)}) collective-permute-start(f32[8,1]{1,0:T(8,128)S(1)} %get-tuple-element.179), channel_id=1, source_target_pairs={{0,1},{1,2},{2,3},{3,4},{4,5},{5,6},{6,7},{7,8},{8,9},{9,10},{10,1... | collective-permute-start | bytes 104 | tf_op jit(solution)/shard_map/ppermute | solution.py:23
  220.4 5.9 %collective-permute-start.22 = (f32[8,127]{1,0:T(8,128)S(1)}, f32[8,127]{1,0:T(8,128)S(1)}, u32[]{:S(2)}, u32[]{:S(2)}) collective-permute-start(f32[8,127]{1,0:T(8,128)S(1)} %get-tuple-element.175), channel_id=1, source_target_pairs={{0,1},{1,2},{2,3},{3,4},{4,5},{5,6},{6,7},{7,8},{8,9},{9,10},{10,1... | collective-permute-start | bytes 12200 | tf_op jit(solution)/shard_map/ppermute | solution.py:23
  231.8 5.6 %collective-permute-start.25 = (f32[8,128]{1,0:T(8,128)S(1)}, f32[8,128]{1,0:T(8,128)S(1)}, u32[]{:S(2)}, u32[]{:S(2)}) collective-permute-start(f32[8,128]{1,0:T(8,128)S(1)} %fusion.77), channel_id=1, source_target_pairs={{1,0},{2,1},{3,2},{4,3},{5,4},{6,5},{7,6},{8,7},{9,8},{10,9},{11,1... | collective-permute-start | bytes 12296 | tf_op jit(solution)/shard_map/ppermute | solution.py:32
  239.0 5.3 collective-permute-start.27
  245.9 6.2 %collective-permute-start.29 = (f32[8,128]{1,0:T(8,128)S(1)}, f32[8,128]{1,0:T(8,128)S(1)}, u32[]{:S(2)}, u32[]{:S(2)}) collective-permute-start(f32[8,128]{1,0:T(8,128)S(1)} %bitcast_add_fusion.36), channel_id=1, source_target_pairs={{4,0},{5,1},{6,2},{7,3},{8,4},{9,5},{10,6},{11,7},{12,8},{13,9},{1... | collective-permute-start | bytes 12296 | tf_op jit(solution)/shard_map/ppermute | solution.py:32
  247.2 5.7 %collective-permute-start.28 = (f32[8,128]{1,0:T(8,128)S(1)}, f32[8,128]{1,0:T(8,128)S(1)}, u32[]{:S(2)}, u32[]{:S(2)}) collective-permute-start(f32[8,128]{1,0:T(8,128)S(1)} %bitcast_add_fusion.36), channel_id=1, source_target_pairs={{0,4},{1,5},{2,6},{3,7},{4,8},{5,9},{6,10},{7,11},{8,12},{9,13},{1... | collective-permute-start | bytes 12296 | tf_op jit(solution)/shard_map/ppermute | solution.py:32
  253.7 12.5 %collective-permute-start.31 = (f32[8,128]{1,0:T(8,128)S(1)}, f32[8,128]{1,0:T(8,128)S(1)}, u32[]{:S(2)}, u32[]{:S(2)}) collective-permute-start(f32[8,128]{1,0:T(8,128)S(1)} %bitcast_add_fusion.34), channel_id=1, source_target_pairs={{8,0},{9,1},{10,2},{11,3},{12,4},{13,5},{14,6},{15,7},{16,8},{17,9... | collective-permute-start | bytes 12296 | tf_op jit(solution)/shard_map/ppermute | solution.py:32
  255.0 12.0 %collective-permute-start.30 = (f32[8,128]{1,0:T(8,128)S(1)}, f32[8,128]{1,0:T(8,128)S(1)}, u32[]{:S(2)}, u32[]{:S(2)}) collective-permute-start(f32[8,128]{1,0:T(8,128)S(1)} %bitcast_add_fusion.34), channel_id=1, source_target_pairs={{0,8},{1,9},{2,10},{3,11},{4,12},{5,13},{6,14},{7,15},{8,16},{9,17... | collective-permute-start | bytes 12296 | tf_op jit(solution)/shard_map/ppermute | solution.py:32
  267.8 14.0 %collective-permute-start.33 = (f32[8,128]{1,0:T(8,128)S(1)}, f32[8,128]{1,0:T(8,128)S(1)}, u32[]{:S(2)}, u32[]{:S(2)}) collective-permute-start(f32[8,128]{1,0:T(8,128)S(1)} %bitcast_add_fusion.32), channel_id=1, source_target_pairs={{16,0},{17,1},{18,2},{19,3},{20,4},{21,5},{22,6},{23,7},{24,8},{25... | collective-permute-start | bytes 12296 | tf_op jit(solution)/shard_map/ppermute | solution.py:32
  269.1 13.5 %collective-permute-start.32 = (f32[8,128]{1,0:T(8,128)S(1)}, f32[8,128]{1,0:T(8,128)S(1)}, u32[]{:S(2)}, u32[]{:S(2)}) collective-permute-start(f32[8,128]{1,0:T(8,128)S(1)} %bitcast_add_fusion.32), channel_id=1, source_target_pairs={{0,16},{1,17},{2,18},{3,19},{4,20},{5,21},{6,22},{7,23},{8,24},{9,... | collective-permute-start | bytes 12296 | tf_op jit(solution)/shard_map/ppermute | solution.py:32
  283.3 8.2 %collective-permute-start.35 = (f32[8,128]{1,0:T(8,128)S(1)}, f32[8,128]{1,0:T(8,128)S(1)}, u32[]{:S(2)}, u32[]{:S(2)}) collective-permute-start(f32[8,128]{1,0:T(8,128)S(1)} %bitcast_add_fusion.30), channel_id=1, source_target_pairs={{32,0},{33,1},{34,2},{35,3},{36,4},{37,5},{38,6},{39,7},{40,8},{41... | collective-permute-start | bytes 12296 | tf_op jit(solution)/shard_map/ppermute | solution.py:32
  284.6 7.6 %collective-permute-start.34 = (f32[8,128]{1,0:T(8,128)S(1)}, f32[8,128]{1,0:T(8,128)S(1)}, u32[]{:S(2)}, u32[]{:S(2)}) collective-permute-start(f32[8,128]{1,0:T(8,128)S(1)} %bitcast_add_fusion.30), channel_id=1, source_target_pairs={{0,32},{1,33},{2,34},{3,35},{4,36},{5,37},{6,38},{7,39},{8,40},{9,... | collective-permute-start | bytes 12296 | tf_op jit(solution)/shard_map/ppermute | solution.py:32
  293.1 17.0 %collective-permute-start.36 = (f32[8,128]{1,0:T(8,128)S(1)}, f32[8,128]{1,0:T(8,128)S(1)}, u32[]{:S(2)}, u32[]{:S(2)}) collective-permute-start(f32[8,128]{1,0:T(8,128)S(1)} %bitcast_add_fusion.28), channel_id=1, source_target_pairs={{0,64},{1,65},{2,66},{3,67},{4,68},{5,69},{6,70},{7,71},{8,72},{9,... | collective-permute-start | bytes 12296 | tf_op jit(solution)/shard_map/ppermute | solution.py:32
  313.1 6.8 %collective-permute-start.39 = (f32[8,128]{1,0:T(8,128)S(1)}, f32[8,128]{1,0:T(8,128)S(1)}, u32[]{:S(2)}, u32[]{:S(2)}) collective-permute-start(f32[8,128]{1,0:T(8,128)S(1)} %bitcast_add_fusion.26), channel_id=1, source_target_pairs={{128,0},{129,1},{130,2},{131,3},{132,4},{133,5},{134,6},{135,7},{1... | collective-permute-start | bytes 12296 | tf_op jit(solution)/shard_map/ppermute | solution.py:32
  314.5 6.2 %collective-permute-start.38 = (f32[8,128]{1,0:T(8,128)S(1)}, f32[8,128]{1,0:T(8,128)S(1)}, u32[]{:S(2)}, u32[]{:S(2)}) collective-permute-start(f32[8,128]{1,0:T(8,128)S(1)} %bitcast_add_fusion.26), channel_id=1, source_target_pairs={{0,128},{1,129},{2,130},{3,131},{4,132},{5,133},{6,134},{7,135},{8... | collective-permute-start | bytes 12296 | tf_op jit(solution)/shard_map/ppermute | solution.py:32
  320.8 13.8 %collective-permute-start.40 = (f32[8,1]{1,0:T(8,128)S(1)}, f32[8,1]{1,0:T(8,128)S(1)}, u32[]{:S(2)}, u32[]{:S(2)}) collective-permute-start(f32[8,1]{1,0:T(8,128)S(1)} %get-tuple-element.173), channel_id=1, source_target_pairs={{0,1},{1,2},{2,3},{3,4},{4,5},{5,6},{6,7},{7,8},{8,9},{9,10},{10,1... | collective-permute-start | bytes 104 | tf_op jit(solution)/shard_map/ppermute | solution.py:23
  382.9 5.8 %collective-permute-start.42 = (f32[8,127]{1,0:T(8,128)S(1)}, f32[8,127]{1,0:T(8,128)S(1)}, u32[]{:S(2)}, u32[]{:S(2)}) collective-permute-start(f32[8,127]{1,0:T(8,128)S(1)} %get-tuple-element.169), channel_id=1, source_target_pairs={{0,1},{1,2},{2,3},{3,4},{4,5},{5,6},{6,7},{7,8},{8,9},{9,10},{10,1... | collective-permute-start | bytes 12200 | tf_op jit(solution)/shard_map/ppermute | solution.py:23
  394.2 5.6 %collective-permute-start.45 = (f32[8,128]{1,0:T(8,128)S(1)}, f32[8,128]{1,0:T(8,128)S(1)}, u32[]{:S(2)}, u32[]{:S(2)}) collective-permute-start(f32[8,128]{1,0:T(8,128)S(1)} %fusion.74), channel_id=1, source_target_pairs={{1,0},{2,1},{3,2},{4,3},{5,4},{6,5},{7,6},{8,7},{9,8},{10,9},{11,1... | collective-permute-start | bytes 12296 | tf_op jit(solution)/shard_map/ppermute | solution.py:32
  400.5 5.3 collective-permute-start.47
  406.6 6.8 %collective-permute-start.49 = (f32[8,128]{1,0:T(8,128)S(1)}, f32[8,128]{1,0:T(8,128)S(1)}, u32[]{:S(2)}, u32[]{:S(2)}) collective-permute-start(f32[8,128]{1,0:T(8,128)S(1)} %bitcast_add_fusion.16), channel_id=1, source_target_pairs={{4,0},{5,1},{6,2},{7,3},{8,4},{9,5},{10,6},{11,7},{12,8},{13,9},{1... | collective-permute-start | bytes 12296 | tf_op jit(solution)/shard_map/ppermute | solution.py:32
  408.5 5.6 %collective-permute-start.48 = (f32[8,128]{1,0:T(8,128)S(1)}, f32[8,128]{1,0:T(8,128)S(1)}, u32[]{:S(2)}, u32[]{:S(2)}) collective-permute-start(f32[8,128]{1,0:T(8,128)S(1)} %bitcast_add_fusion.16), channel_id=1, source_target_pairs={{0,4},{1,5},{2,6},{3,7},{4,8},{5,9},{6,10},{7,11},{8,12},{9,13},{1... | collective-permute-start | bytes 12296 | tf_op jit(solution)/shard_map/ppermute | solution.py:32
  414.1 13.1 %collective-permute-start.51 = (f32[8,128]{1,0:T(8,128)S(1)}, f32[8,128]{1,0:T(8,128)S(1)}, u32[]{:S(2)}, u32[]{:S(2)}) collective-permute-start(f32[8,128]{1,0:T(8,128)S(1)} %bitcast_add_fusion.14), channel_id=1, source_target_pairs={{8,0},{9,1},{10,2},{11,3},{12,4},{13,5},{14,6},{15,7},{16,8},{17,9... | collective-permute-start | bytes 12296 | tf_op jit(solution)/shard_map/ppermute | solution.py:32
  416.1 11.9 %collective-permute-start.50 = (f32[8,128]{1,0:T(8,128)S(1)}, f32[8,128]{1,0:T(8,128)S(1)}, u32[]{:S(2)}, u32[]{:S(2)}) collective-permute-start(f32[8,128]{1,0:T(8,128)S(1)} %bitcast_add_fusion.14), channel_id=1, source_target_pairs={{0,8},{1,9},{2,10},{3,11},{4,12},{5,13},{6,14},{7,15},{8,16},{9,17... | collective-permute-start | bytes 12296 | tf_op jit(solution)/shard_map/ppermute | solution.py:32
  428.0 14.3 %collective-permute-start.53 = (f32[8,128]{1,0:T(8,128)S(1)}, f32[8,128]{1,0:T(8,128)S(1)}, u32[]{:S(2)}, u32[]{:S(2)}) collective-permute-start(f32[8,128]{1,0:T(8,128)S(1)} %bitcast_add_fusion.12), channel_id=1, source_target_pairs={{16,0},{17,1},{18,2},{19,3},{20,4},{21,5},{22,6},{23,7},{24,8},{25... | collective-permute-start | bytes 12296 | tf_op jit(solution)/shard_map/ppermute | solution.py:32
  429.3 13.7 %collective-permute-start.52 = (f32[8,128]{1,0:T(8,128)S(1)}, f32[8,128]{1,0:T(8,128)S(1)}, u32[]{:S(2)}, u32[]{:S(2)}) collective-permute-start(f32[8,128]{1,0:T(8,128)S(1)} %bitcast_add_fusion.12), channel_id=1, source_target_pairs={{0,16},{1,17},{2,18},{3,19},{4,20},{5,21},{6,22},{7,23},{8,24},{9,... | collective-permute-start | bytes 12296 | tf_op jit(solution)/shard_map/ppermute | solution.py:32
  443.0 9.6 %collective-permute-start.55 = (f32[8,128]{1,0:T(8,128)S(1)}, f32[8,128]{1,0:T(8,128)S(1)}, u32[]{:S(2)}, u32[]{:S(2)}) collective-permute-start(f32[8,128]{1,0:T(8,128)S(1)} %bitcast_add_fusion.10), channel_id=1, source_target_pairs={{32,0},{33,1},{34,2},{35,3},{36,4},{37,5},{38,6},{39,7},{40,8},{41... | collective-permute-start | bytes 12296 | tf_op jit(solution)/shard_map/ppermute | solution.py:32
  445.7 7.7 %collective-permute-start.54 = (f32[8,128]{1,0:T(8,128)S(1)}, f32[8,128]{1,0:T(8,128)S(1)}, u32[]{:S(2)}, u32[]{:S(2)}) collective-permute-start(f32[8,128]{1,0:T(8,128)S(1)} %bitcast_add_fusion.10), channel_id=1, source_target_pairs={{0,32},{1,33},{2,34},{3,35},{4,36},{5,37},{6,38},{7,39},{8,40},{9,... | collective-permute-start | bytes 12296 | tf_op jit(solution)/shard_map/ppermute | solution.py:32
  453.3 18.9 %collective-permute-start.56 = (f32[8,128]{1,0:T(8,128)S(1)}, f32[8,128]{1,0:T(8,128)S(1)}, u32[]{:S(2)}, u32[]{:S(2)}) collective-permute-start(f32[8,128]{1,0:T(8,128)S(1)} %bitcast_add_fusion.8), channel_id=1, source_target_pairs={{0,64},{1,65},{2,66},{3,67},{4,68},{5,69},{6,70},{7,71},{8,72},{9,... | collective-permute-start | bytes 12296 | tf_op jit(solution)/shard_map/ppermute | solution.py:32
  475.3 8.3 %collective-permute-start.59 = (f32[8,128]{1,0:T(8,128)S(1)}, f32[8,128]{1,0:T(8,128)S(1)}, u32[]{:S(2)}, u32[]{:S(2)}) collective-permute-start(f32[8,128]{1,0:T(8,128)S(1)} %bitcast_add_fusion.6), channel_id=1, source_target_pairs={{128,0},{129,1},{130,2},{131,3},{132,4},{133,5},{134,6},{135,7},{1... | collective-permute-start | bytes 12296 | tf_op jit(solution)/shard_map/ppermute | solution.py:32
  478.1 6.2 %collective-permute-start.58 = (f32[8,128]{1,0:T(8,128)S(1)}, f32[8,128]{1,0:T(8,128)S(1)}, u32[]{:S(2)}, u32[]{:S(2)}) collective-permute-start(f32[8,128]{1,0:T(8,128)S(1)} %bitcast_add_fusion.6), channel_id=1, source_target_pairs={{0,128},{1,129},{2,130},{3,131},{4,132},{5,133},{6,134},{7,135},{8... | collective-permute-start | bytes 12296 | tf_op jit(solution)/shard_map/ppermute | solution.py:32
  484.5 13.9 %collective-permute-start.60 = (f32[8,1]{1,0:T(8,128)S(1)}, f32[8,1]{1,0:T(8,128)S(1)}, u32[]{:S(2)}, u32[]{:S(2)}) collective-permute-start(f32[8,1]{1,0:T(8,128)S(1)} %get-tuple-element.167), channel_id=1, source_target_pairs={{0,1},{1,2},{2,3},{3,4},{4,5},{5,6},{6,7},{7,8},{8,9},{9,10},{10,1... | collective-permute-start | bytes 104 | tf_op jit(solution)/shard_map/ppermute | solution.py:23
  (22 other events, 799.9 us)
where the time goes:
time: 555 us; the launch traced here: 551 us
  starting transfers between devices  297 us (54%)
  blocking collectives  167 us (30%)
  other arithmetic  39.3 us (7%)
  waiting for transfers between devices  29.6 us (5%)
  local copies, waits for them, and re-layouts  8.88 us (2%)
  between operations  8.41 us (2%)
    ppermute x48, starting transfers between devices, from_behind(): return lax.ppermute(x, axis, pairs)  229 us
    psum x16, blocking collectives, one_axis_at_a_time(): return functools.reduce(lax.psum, axes, x)  167 us
    ppermute x7, starting transfers between devices, padded_2(): before = lax.ppermute(last, axis, up)  53.2 us
    dot_general x101, other arithmetic, blockmul(): jnp.einsum('abi,bi->ai', blocks, field, precision=lax.Precision.HIGHEST)  26.3 us
    ppermute x7, waiting for transfers between devices, padded_2(): after = lax.ppermute(initial, axis, down)  17.8 us
    ppermute x7, starting transfers between devices, padded_2(): after = lax.ppermute(initial, axis, down)  14.7 us
    ppermute x48, waiting for transfers between devices, from_behind(): return lax.ppermute(x, axis, pairs)  11.8 us
  transfers between devices with their start and end apart: 62, of which 16 were waited for; matrix products, arithmetic and copies ran while one was open for 3% of the time, Pallas kernels for 0%

commit v1 on v0

v1 whole, which is shorter than its diff:
```python
import functools

import jax
import jax.numpy as jnp
from jax import lax
from jax.experimental import pallas as pl
from jax.experimental.pallas import tpu as pltpu
from jax.sharding import PartitionSpec as P

ITERS = 3
EPS = 1e-06
DEV = 256
ROWS = 128
COUNT = 8 * DEV * ROWS
F32 = jnp.float32
NEAR = 7
LOWS = (-3, -2, -1, 1, 2, 3)


def kernel(
    r_hbm, dg_hbm, bl_hbm, ab_hbm, lo_hbm, up_hbm, fb_hbm,
    basis_ref, hess_ref,
    rv, av, fv, cf,
    near_c, near_a, c7, c9, c11, c12, c13,
    xs, bs, gr,
    src1, src2, src3, srct, srcz, srcp,
    h1, h2, h3, ht, hz, hp,
    lsem, msend, mrecv, rsend, rrecv,
):
    d = lax.axis_index("chain")
    t = lax.rem(d, 16)
    line = d - t

    def dev(offset):
        return lax.rem(d + (offset % DEV), DEV)

    def in_line(offset):
        return line + lax.rem(t + (offset % 16), 16)

    loads = [
        pltpu.make_async_copy(r_hbm, rv, lsem.at[0]),
        pltpu.make_async_copy(lo_hbm, cf.at[:, 0], lsem.at[1]),
        pltpu.make_async_copy(up_hbm, cf.at[:, 1], lsem.at[2]),
        pltpu.make_async_copy(dg_hbm, av.at[0], lsem.at[3]),
        pltpu.make_async_copy(bl_hbm, av.at[1], lsem.at[4]),
        pltpu.make_async_copy(ab_hbm, av.at[2], lsem.at[5]),
        pltpu.make_async_copy(fb_hbm, fv, lsem.at[6]),
    ]
    for load in loads:
        load.start()

    partners = [dev(o) for o in (-12, -8, -4, -3, -2, -1, 1, 2, 3, 4, 8, 12)]
    partners += [dev(16 * o) for o in range(1, 16)]
    partners += [in_line(o) for o in range(1, 16)]
    barrier = pltpu.get_barrier_semaphore()
    for other in partners:
        pl.semaphore_signal(barrier, inc=1, device_id=(other,), device_id_type=pl.DeviceIdType.MESH)
    pl.semaphore_wait(barrier, len(partners))

    def send(src, dst, ssem, rsem, other):
        pltpu.make_async_remote_copy(
            src_ref=src, dst_ref=dst, send_sem=ssem, recv_sem=rsem,
            device_id=(other,), device_id_type=pl.DeviceIdType.MESH,
        ).start()

    def drain(buf, sem):
        pltpu.make_async_copy(buf, buf, sem).wait()

    for load in loads:
        load.wait()

    send(rv, h1.at[0, 1], rsend.at[0, 0], rrecv.at[0, 0], dev(-1))
    send(rv, h1.at[0, 0], rsend.at[0, 0], rrecv.at[0, 0], dev(1))
    send(cf.at[pl.ds(0, 6)], near_c.at[1], msend.at[0], mrecv.at[0], dev(-1))
    send(cf.at[pl.ds(0, 6)], near_c.at[0], msend.at[0], mrecv.at[0], dev(1))
    send(cf.at[7], c7.at[1], msend.at[1], mrecv.at[1], dev(-2))
    send(cf.at[7], c7.at[0], msend.at[1], mrecv.at[1], dev(2))
    send(cf.at[9], c9.at[1], msend.at[2], mrecv.at[2], dev(-8))
    send(cf.at[9], c9.at[0], msend.at[2], mrecv.at[2], dev(8))
    for p in range(2, 16, 2):
        send(cf.at[11], c11.at[p // 2 - 1], msend.at[3], mrecv.at[3], dev(-16 * p))
    for p in range(4, 16, 4):
        send(cf.at[12], c12.at[p // 4 - 1], msend.at[4], mrecv.at[4], dev(-16 * p))
    send(cf.at[13], c13, msend.at[5], mrecv.at[5], dev(-16 * 8))
    send(av, near_a.at[1], msend.at[6], mrecv.at[6], dev(-1))
    send(av, near_a.at[0], msend.at[6], mrecv.at[6], dev(1))

    lane = lax.broadcasted_iota(jnp.int32, (8, ROWS), 1)
    sub = lax.broadcasted_iota(jnp.int32, (8, ROWS), 0)

    def flag(cond):
        return jnp.where(cond, 1.0, 0.0).astype(F32)

    has_below, has_above = flag(d >= 1), flag(d <= DEV - 2)

    def mul(blocks, v):
        total = blocks[pl.ds(0, 8, stride=8), :] * v[0:1]
        for b in range(1, 8):
            total = total + blocks[pl.ds(b, 8, stride=8), :] * v[b : b + 1]
        return total

    def step(coef, x, below, above):
        return x + mul(coef.at[0], below) + mul(coef.at[1], above)

    def down(u, prev, s):
        return jnp.where(lane < s, pltpu.roll(prev, s, 1), pltpu.roll(u, s, 1))

    def upward(u, following, s):
        return jnp.where(
            lane >= ROWS - s, pltpu.roll(following, ROWS - s, 1), pltpu.roll(u, ROWS - s, 1)
        )

    def far_level(coef, x, below, above, p, by, scale=1, size=DEV):
        place = lax.rem(d + (p % DEV), DEV)
        return step(
            coef, x, below * flag(place >= by), above * flag(place + by <= DEV - 1)
        )

    def send_sums(block, j):
        srcz[j] = block
        for o in range(1, 16):
            send(srcz.at[j], hz.at[j, o - 1], rsend.at[j, 4], rrecv.at[j, 4], in_line(-o))

    def pass_sums(j):
        drain(hz.at[j], rrecv.at[j, 4])
        total = srcz[j]
        for o in range(15):
            total = total + hz[j, o]
        srcp[j] = total
        for o in range(1, 16):
            send(srcp.at[j], hp.at[j, o - 1], rsend.at[j, 5], rrecv.at[j, 5], dev(-16 * o))

    def take_sums(j):
        drain(hp.at[j], rrecv.at[j, 5])
        total = srcp[j]
        for o in range(15):
            total = total + hp[j, o]
        return jnp.sum(total, axis=1, keepdims=True) * (1.0 / COUNT) + jnp.zeros((8, ROWS), F32)

    def finish(j, x, hess):
        sums = take_sums(j)
        h = [sums[i : i + 1] for i in range(3)]
        squares = sums[3:4]
        gr[lax.max(j - 1, 0)] = sums
        for i in range(3):
            squares = squares - 2.0 * (h[i] * h[i])
        for c in range(3):
            g = gr[c]
            for i in range(c + 1):
                squares = squares + (1.0 if i == c else 2.0) * (h[c] * h[i]) * g[4 + i : 5 + i]
        length = jnp.sqrt(jnp.maximum(squares, 0.0) + EPS)
        inverse = 1.0 / length
        new = x
        for i in range(3):
            new = new - h[i] * bs[i]
        new = new * inverse
        column = jnp.where(sub < 3, sums, 0.0)
        column = jnp.where(sub == j, length + jnp.zeros((8, ROWS), F32), column)
        hess = jnp.where(lane == j - 1, column, hess)
        return h, inverse, new, hess

    zero = jnp.zeros((8, ROWS), F32)
    for i in range(4):
        bs[i] = zero
    for i in range(3):
        gr[i] = zero
    for i in range(4):
        for c in range(3):
            xs[i, c] = zero

    r = rv[...]
    send_sums(jnp.where(sub == 3, jnp.sum(r * r, axis=0, keepdims=True) + zero, 0.0), 0)
    drain(h1.at[0], rrecv.at[0, 0])
    xs[0, 0] = h1[0, 0] * has_below
    xs[0, 1] = r
    xs[0, 2] = h1[0, 1] * has_above
    drain(near_c, mrecv.at[0])

    def body(j, hess):
        u = [xs[j, 0], xs[j, 1], xs[j, 2]]
        for level in range(NEAR):
            s = 2**level
            mid = step(cf.at[level], u[1], down(u[1], u[0], s), upward(u[1], u[2], s))
            if level < NEAR - 1:
                left = step(
                    near_c.at[0, level], u[0], down(u[0], u[0], s), upward(u[0], u[1], s)
                ) * has_below
                right = step(
                    near_c.at[1, level], u[2], down(u[2], u[1], s), upward(u[2], u[2], s)
                ) * has_above
                u = [left, mid, right]
            else:
                u = [None, mid, None]
        x = u[1]

        def group(x, src, got, slot, near_coef, level, by):
            src[j] = x
            for k, o in enumerate(LOWS):
                send(src.at[j], got.at[j, k], rsend.at[j, slot], rrecv.at[j, slot], dev(-o * by))
            drain(got.at[j], rrecv.at[j, slot])
            f = {o: got[j, k] for k, o in enumerate(LOWS)}
            f[0] = x
            y = {
                0: far_level(cf.at[level], f[0], f[-1], f[1], 0, by),
                -2: far_level(near_coef.at[0], f[-2], f[-3], f[-1], -2 * by, by),
                2: far_level(near_coef.at[1], f[2], f[1], f[3], 2 * by, by),
            }
            return far_level(cf.at[level + 1], y[0], y[-2], y[2], 0, 2 * by)

        @pl.when(j == 0)
        def _():
            drain(c7, mrecv.at[1])

        x = group(x, src2, h2, 1, c7, 7, 1)

        @pl.when(j == 0)
        def _():
            drain(c9, mrecv.at[2])

        x = group(x, src3, h3, 2, c9, 9, 4)

        srct[j] = x
        for o in range(1, 16):
            send(srct.at[j], ht.at[j, o - 1], rsend.at[j, 3], rrecv.at[j, 3], dev(-16 * o))
        pass_sums(j)

        @pl.when(j == 0)
        def _():
            drain(c11, mrecv.at[3])
            drain(c12, mrecv.at[4])
            drain(c13, mrecv.at[5])

        drain(ht.at[j], rrecv.at[j, 3])
        f = [x] + [ht[j, o] for o in range(15)]

        def top(coef, field, p, by):
            return far_level(
                coef, field[p], field[(p - by) % 16], field[(p + by) % 16], 16 * p, 16 * by
            )

        y1 = {p: top(cf.at[11] if p == 0 else c11.at[p // 2 - 1], f, p, 1) for p in range(0, 16, 2)}
        y2 = {p: top(cf.at[12] if p == 0 else c12.at[p // 4 - 1], y1, p, 2) for p in range(0, 16, 4)}
        y3 = {p: top(cf.at[13] if p == 0 else c13, y2, p, 4) for p in (0, 8)}
        x = top(cf.at[14], y3, 0, 8)
        x = x + mul(fv, x)

        src1[j] = x
        send(src1.at[j], h1.at[j + 1, 1], rsend.at[j + 1, 0], rrecv.at[j + 1, 0], dev(-1))
        send(src1.at[j], h1.at[j + 1, 0], rsend.at[j + 1, 0], rrecv.at[j + 1, 0], dev(1))

        h, inverse, new, hess = finish(j, xs[j, 1], hess)
        bs[j] = new
        basis_ref[j] = new

        @pl.when(j == 0)
        def _():
            drain(near_a, mrecv.at[6])

        drain(h1.at[j + 1], rrecv.at[j + 1, 0])
        cols = [h1[j + 1, 0] * has_below, x, h1[j + 1, 1] * has_above]
        for c, (coef, mask) in enumerate(
            ((near_a.at[0], has_below), (av, None), (near_a.at[1], has_above))
        ):
            v = 2.0 * cols[c] + mul(coef.at[0], cols[c])
            v = v + mul(coef.at[1], down(cols[c], cols[max(c - 1, 0)], 1))
            v = v + mul(coef.at[2], upward(cols[c], cols[min(c + 1, 2)], 1))
            for i in range(2):
                v = v - h[i] * xs[i + 1, c]
            v = v * inverse
            xs[j + 1, c] = v if mask is None else v * mask

        w = xs[j + 1, 1]
        sums = zero
        rows = [bs[0] * w, bs[1] * w, bs[2] * w, w * w, bs[0] * new, bs[1] * new, bs[2] * new]
        for i, row in enumerate(rows):
            sums = jnp.where(sub == i, jnp.sum(row, axis=0, keepdims=True) + zero, sums)
        send_sums(sums, j + 1)
        return hess

    hess = lax.fori_loop(0, ITERS, body, zero)
    pass_sums(ITERS)
    _, _, new, hess = finish(ITERS, xs[ITERS, 1], hess)
    basis_ref[ITERS] = new
    hess_ref[...] = hess

    drain(near_c, msend.at[0])
    drain(c7, msend.at[1])
    drain(c9, msend.at[2])
    drain(c11, msend.at[3])
    drain(c12, msend.at[4])
    drain(c13, msend.at[5])
    drain(near_a, msend.at[6])
    for j in range(ITERS + 1):
        drain(h1.at[j], rsend.at[j, 0])
        drain(hz.at[j], rsend.at[j, 4])
        drain(hp.at[j], rsend.at[j, 5])
        if j < ITERS:
            drain(h2.at[j], rsend.at[j, 1])
            drain(h3.at[j], rsend.at[j, 2])
            drain(ht.at[j], rsend.at[j, 3])


def on_device(right_side, diag_block, below_block, above_block, lower_level, upper_level, final_block):
    block = (64, ROWS)
    tile = (8, ROWS)
    vmem = lambda *lead: pltpu.VMEM(lead, F32)
    basis, hess = pl.pallas_call(
        kernel,
        out_shape=(
            jax.ShapeDtypeStruct((ITERS + 1, 8, ROWS), F32),
            jax.ShapeDtypeStruct(tile, F32),
        ),
        in_specs=[pl.BlockSpec(memory_space=pl.ANY)] * 7,
        out_specs=(pl.BlockSpec(memory_space=pltpu.VMEM), pl.BlockSpec(memory_space=pltpu.VMEM)),
        scratch_shapes=[
            vmem(*tile), vmem(3, *block), vmem(*block), vmem(15, 2, *block),
            vmem(2, 6, 2, *block), vmem(2, 3, *block), vmem(2, 2, *block), vmem(2, 2, *block),
            vmem(7, 2, *block), vmem(3, 2, *block), vmem(2, *block),
            vmem(4, 3, *tile), vmem(4, *tile), vmem(3, *tile),
            vmem(3, *tile), vmem(3, *tile), vmem(3, *tile), vmem(3, *tile),
            vmem(4, *tile), vmem(4, *tile),
            vmem(4, 2, *tile), vmem(3, 6, *tile), vmem(3, 6, *tile), vmem(3, 15, *tile),
            vmem(4, 15, *tile), vmem(4, 15, *tile),
            pltpu.SemaphoreType.DMA((7,)),
            pltpu.SemaphoreType.DMA((7,)),
            pltpu.SemaphoreType.DMA((7,)),
            pltpu.SemaphoreType.DMA((4, 6)),
            pltpu.SemaphoreType.DMA((4, 6)),
        ],
        compiler_params=pltpu.CompilerParams(collective_id=0, has_side_effects=True),
    )(
        right_side,
        diag_block.reshape(block),
        below_block.reshape(block),
        above_block.reshape(block),
        lower_level.reshape((15,) + block),
        upper_level.reshape((15,) + block),
        final_block.reshape(block),
    )
    return basis, hess[: ITERS + 1, :ITERS]


def solution(mesh):
    blocks = P(None, None, "chain")
    levels = P(None, None, None, "chain")
    return jax.shard_map(
        on_device,
        mesh=mesh,
        in_specs=(P(None, "chain"), blocks, blocks, blocks, levels, levels, blocks),
        out_specs=(P(None, None, "chain"), P()),
        check_vma=False,
    )
```

time: 555 us -> 99 us (0.18)
  starting transfers between devices: 297 us -> 0 us
  blocking collectives: 167 us -> 0 us
  Pallas kernels: 0 us -> 95.6 us
  other arithmetic: 39.3 us -> 0 us
  waiting for transfers between devices: 29.6 us -> 0 us
  between operations: 8.41 us -> 0.64 us
  local copies, waits for them, and re-layouts: 8.88 us -> 2.57 us
    ppermute x62 -> x0, starting transfers between devices: 297 us -> none  [the longest x48 229 us: from_behind(): return lax.ppermute(x, axis, pairs)]
    psum x16 -> x0, blocking collectives: 167 us -> none  [one_axis_at_a_time(): return functools.reduce(lax.psum, axes, x)]
    pallas_call x0 -> x1, Pallas kernels: none -> 95.6 us  [on_device(): pl.pallas_call(kernel, out_shape=(jax.ShapeDtypeStruct((ITERS + 1, 8, ROW...]
    ppermute x62 -> x0, waiting for transfers between devices: 29.6 us -> none  [the longest x7 17.8 us: padded_2(): after = lax.ppermute(initial, axis, down)]
    dot_general x102 -> x0, other arithmetic: 26.9 us -> none  [the longest x101 26.3 us: blockmul(): jnp.einsum('abi,bi->ai', blocks, field, precision=lax.Precision.HIGHEST)]
    another operation x10 -> x0, other arithmetic: 5.66 us -> none
  transfers between devices with their start and end apart: 62 -> 0, of which waited for: 16 -> 0; matrix products, arithmetic and copies ran while one was open for 3% -> 0% of each run, Pallas kernels for 0% -> 0%
where the time goes in v1:
time: 99 us; the launch traced here: 98.8 us
  Pallas kernels  95.6 us (97%)
  local copies, waits for them, and re-layouts  2.57 us (3%)
    pallas_call x1, Pallas kernels, on_device(): pl.pallas_call(kernel, out_shape=(jax.ShapeDtypeStruct((ITERS + 1, 8, ROW...  95.6 us

profile of v1, /device:TPU:1, one launch (start us, length us, event | category | flops | bytes accessed | tf_op | source)
XLA Modules:
  0.0 98.8 jit_solution(8070147659570612725)
XLA Ops:
  0.6 95.6 %shard_map.86 = (f32[4,8,128]{2,1,0:T(8,128)}, f32[8,128]{1,0:T(8,128)}) custom-call(f32[8,128]{1,0:T(8,128)} %r_hbm.1, f32[64,128]{1,0:T(8,128)} %bitcast.8, f32[64,128]{1,0:T(8,128)} %bitcast.9, f32[64,128]{1,0:T(8,128)} %bitcast.10, f32[15,64,128]{2,1,0:T(8,128)} %bitcast.6, f32[15,64,128]{2,1,0:T(8,128)} %bitcast.7, f32[64,128]{1,0:T(8,128)} %bitcast.11), custom_call_target="tpu_custom_call" | custom-call | tf_op jit(solution)/shard_map/pallas_call | solution.py:307
  96.2 1.2 %slice.3 = f32[4,3]{1,0:T(4,128)} slice(f32[8,128]{1,0:T(8,128)} %get-tuple-element.5), slice={[0:4], [0:3]} | slice | bytes 96 | tf_op jit(solution)/shard_map/slice | solution.py:340
  97.5 1.3 %copy.10 = f32[4,8,128]{2,1,0:T(8,128)} copy(f32[4,8,128]{2,1,0:T(8,128)} %get-tuple-element.8) | data formatting | bytes 32768

commit v2 on v1

--- a/solution.py
+++ b/solution.py
@@ -73,20 +73,31 @@
     send(rv, h1.at[0, 0], rsend.at[0, 0], rrecv.at[0, 0], dev(1))
     send(cf.at[pl.ds(0, 6)], near_c.at[1], msend.at[0], mrecv.at[0], dev(-1))
     send(cf.at[pl.ds(0, 6)], near_c.at[0], msend.at[0], mrecv.at[0], dev(1))
-    send(cf.at[7], c7.at[1], msend.at[1], mrecv.at[1], dev(-2))
-    send(cf.at[7], c7.at[0], msend.at[1], mrecv.at[1], dev(2))
-    send(cf.at[9], c9.at[1], msend.at[2], mrecv.at[2], dev(-8))
-    send(cf.at[9], c9.at[0], msend.at[2], mrecv.at[2], dev(8))
-    for p in range(2, 16, 2):
-        send(cf.at[11], c11.at[p // 2 - 1], msend.at[3], mrecv.at[3], dev(-16 * p))
-    for p in range(4, 16, 4):
-        send(cf.at[12], c12.at[p // 4 - 1], msend.at[4], mrecv.at[4], dev(-16 * p))
-    send(cf.at[13], c13, msend.at[5], mrecv.at[5], dev(-16 * 8))
-    send(av, near_a.at[1], msend.at[6], mrecv.at[6], dev(-1))
-    send(av, near_a.at[0], msend.at[6], mrecv.at[6], dev(1))
+
+    def send_low(first):
+        if first:
+            send(cf.at[7], c7.at[1], msend.at[1], mrecv.at[1], dev(-2))
+            send(cf.at[7], c7.at[0], msend.at[1], mrecv.at[1], dev(2))
+        else:
+            send(cf.at[9], c9.at[1], msend.at[2], mrecv.at[2], dev(-8))
+            send(cf.at[9], c9.at[0], msend.at[2], mrecv.at[2], dev(8))
+
+    def send_top():
+        for p in range(2, 16, 2):
+            send(cf.at[11], c11.at[p // 2 - 1], msend.at[3], mrecv.at[3], dev(-16 * p))
+        for p in range(4, 16, 4):
+            send(cf.at[12], c12.at[p // 4 - 1], msend.at[4], mrecv.at[4], dev(-16 * p))
+        send(cf.at[13], c13, msend.at[5], mrecv.at[5], dev(-16 * 8))
+
+    def send_operator():
+        send(av, near_a.at[1], msend.at[6], mrecv.at[6], dev(-1))
+        send(av, near_a.at[0], msend.at[6], mrecv.at[6], dev(1))
+
+    send_low(True)
 
     lane = lax.broadcasted_iota(jnp.int32, (8, ROWS), 1)
     sub = lax.broadcasted_iota(jnp.int32, (8, ROWS), 0)
+    mine = (lane >= 16 * sub) & (lane < 16 * sub + 16)
 
     def flag(cond):
         return jnp.where(cond, 1.0, 0.0).astype(F32)
@@ -117,25 +128,27 @@
         )
 
     def send_sums(block, j):
-        srcz[j] = block
+        block = block + pltpu.roll(block, 64, 1)
+        block = block + pltpu.roll(block, 32, 1)
+        block = block + pltpu.roll(block, 16, 1)
+        row = jnp.sum(jnp.where(mine, block, 0.0), axis=0, keepdims=True)
+        hz[j, pl.ds(15, 1)] = row
+        srcz[j] = row
         for o in range(1, 16):
-            send(srcz.at[j], hz.at[j, o - 1], rsend.at[j, 4], rrecv.at[j, 4], in_line(-o))
+            send(srcz.at[j], hz.at[j, pl.ds(o - 1, 1)], rsend.at[j, 4], rrecv.at[j, 4], in_line(-o))
 
     def pass_sums(j):
-        drain(hz.at[j], rrecv.at[j, 4])
-        total = srcz[j]
-        for o in range(15):
-            total = total + hz[j, o]
-        srcp[j] = total
+        drain(hz.at[j, pl.ds(0, 15)], rrecv.at[j, 4])
+        row = jnp.sum(hz[j], axis=0, keepdims=True)
+        hp[j, pl.ds(15, 1)] = row
+        srcp[j] = row
         for o in range(1, 16):
-            send(srcp.at[j], hp.at[j, o - 1], rsend.at[j, 5], rrecv.at[j, 5], dev(-16 * o))
+            send(srcp.at[j], hp.at[j, pl.ds(o - 1, 1)], rsend.at[j, 5], rrecv.at[j, 5], dev(-16 * o))
 
     def take_sums(j):
-        drain(hp.at[j], rrecv.at[j, 5])
-        total = srcp[j]
-        for o in range(15):
-            total = total + hp[j, o]
-        return jnp.sum(total, axis=1, keepdims=True) * (1.0 / COUNT) + jnp.zeros((8, ROWS), F32)
+        drain(hp.at[j, pl.ds(0, 15)], rrecv.at[j, 5])
+        total = jnp.sum(hp[j], axis=0, keepdims=True)
+        return jnp.sum(jnp.where(mine, total, 0.0), axis=1, keepdims=True) * (1.0 / COUNT) + jnp.zeros((8, ROWS), F32)
 
     def finish(j, x, hess):
         sums = take_sums(j)
@@ -193,10 +206,11 @@
                 u = [None, mid, None]
         x = u[1]
 
-        def group(x, src, got, slot, near_coef, level, by):
+        def group(x, src, got, slot, near_coef, level, by, later):
             src[j] = x
             for k, o in enumerate(LOWS):
                 send(src.at[j], got.at[j, k], rsend.at[j, slot], rrecv.at[j, slot], dev(-o * by))
+            pl.when(j == 0)(later)
             drain(got.at[j], rrecv.at[j, slot])
             f = {o: got[j, k] for k, o in enumerate(LOWS)}
             f[0] = x
@@ -207,17 +221,17 @@
             }
             return far_level(cf.at[level + 1], y[0], y[-2], y[2], 0, 2 * by)
 
-        @pl.when(j == 0)
-        def _():
+        def after_first():
+            send_low(False)
+            send_top()
             drain(c7, mrecv.at[1])
 
-        x = group(x, src2, h2, 1, c7, 7, 1)
-
-        @pl.when(j == 0)
-        def _():
+        def after_second():
+            send_operator()
             drain(c9, mrecv.at[2])
 
-        x = group(x, src3, h3, 2, c9, 9, 4)
+        x = group(x, src2, h2, 1, c7, 7, 1, after_first)
+        x = group(x, src3, h3, 2, c9, 9, 4, after_second)
 
         srct[j] = x
         for o in range(1, 16):
@@ -292,12 +306,17 @@
     drain(near_a, msend.at[6])
     for j in range(ITERS + 1):
         drain(h1.at[j], rsend.at[j, 0])
-        drain(hz.at[j], rsend.at[j, 4])
-        drain(hp.at[j], rsend.at[j, 5])
+        drain(hz.at[j, pl.ds(0, 15)], rsend.at[j, 4])
+        drain(hp.at[j, pl.ds(0, 15)], rsend.at[j, 5])
         if j < ITERS:
             drain(h2.at[j], rsend.at[j, 1])
             drain(h3.at[j], rsend.at[j, 2])
             drain(ht.at[j], rsend.at[j, 3])
+
+
+def hand_out(basis_ref, hess_ref, basis_out, hess_out):
+    basis_out[...] = basis_ref[...]
+    hess_out[...] = hess_ref[: ITERS + 1, :ITERS]
 
 
 def on_device(right_side, diag_block, below_block, above_block, lower_level, upper_level, final_block):
@@ -318,9 +337,9 @@
             vmem(7, 2, *block), vmem(3, 2, *block), vmem(2, *block),
             vmem(4, 3, *tile), vmem(4, *tile), vmem(3, *tile),
             vmem(3, *tile), vmem(3, *tile), vmem(3, *tile), vmem(3, *tile),
-            vmem(4, *tile), vmem(4, *tile),
+            vmem(4, 1, ROWS), vmem(4, 1, ROWS),
             vmem(4, 2, *tile), vmem(3, 6, *tile), vmem(3, 6, *tile), vmem(3, 15, *tile),
-            vmem(4, 15, *tile), vmem(4, 15, *tile),
+            vmem(4, 16, ROWS), vmem(4, 16, ROWS),
             pltpu.SemaphoreType.DMA((7,)),
             pltpu.SemaphoreType.DMA((7,)),
             pltpu.SemaphoreType.DMA((7,)),
@@ -337,7 +356,15 @@
         upper_level.reshape((15,) + block),
         final_block.reshape(block),
     )
-    return basis, hess[: ITERS + 1, :ITERS]
+    return pl.pallas_call(
+        hand_out,
+        out_shape=(
+            jax.ShapeDtypeStruct((ITERS + 1, 8, ROWS), F32),
+            jax.ShapeDtypeStruct((ITERS + 1, ITERS), F32),
+        ),
+        in_specs=[pl.BlockSpec(memory_space=pltpu.VMEM)] * 2,
+        out_specs=(pl.BlockSpec(memory_space=pltpu.VMEM), pl.BlockSpec(memory_space=pltpu.VMEM)),
+    )(basis, hess)
 
 
 def solution(mesh):

time: 99 us -> 93.4 us (0.943)
  Pallas kernels: 95.6 us -> 92.6 us
  local copies, waits for them, and re-layouts: 2.57 us -> 0 us
    pallas_call x1, Pallas kernels: 95.6 us -> 91.2 us  [on_device(): pl.pallas_call(kernel, out_shape=(jax.ShapeDtypeStruct((ITERS + 1, 8, ROW...]
    pallas_call x0 -> x1, Pallas kernels: none -> 1.33 us  [on_device(): pl.pallas_call(hand_out, out_shape=(jax.ShapeDtypeStruct((ITERS + 1, 8, R...]
    unnamed x1 -> x0, local copies, waits for them, and re-layouts: 1.32 us -> none
    slice x1 -> x0, local copies, waits for them, and re-layouts: 1.25 us -> none  [on_device(): return (basis, hess[:ITERS + 1, :ITERS])]
where the time goes in v2:
time: 93.4 us; the launch traced here: 93.2 us
  Pallas kernels  92.6 us (99%)
    pallas_call x1, Pallas kernels, on_device(): pl.pallas_call(kernel, out_shape=(jax.ShapeDtypeStruct((ITERS + 1, 8, ROW...  91.2 us

profile of v2, /device:TPU:1, one launch (start us, length us, event | category | flops | bytes accessed | tf_op | source)
XLA Modules:
  0.0 93.2 jit_solution(17171785613113470954)
XLA Ops:
  0.6 91.2 %shard_map.86 = (f32[4,8,128]{2,1,0:T(8,128)}, f32[8,128]{1,0:T(8,128)}) custom-call(f32[8,128]{1,0:T(8,128)} %r_hbm.1, f32[64,128]{1,0:T(8,128)} %bitcast.8, f32[64,128]{1,0:T(8,128)} %bitcast.9, f32[64,128]{1,0:T(8,128)} %bitcast.10, f32[15,64,128]{2,1,0:T(8,128)} %bitcast.6, f32[15,64,128]{2,1,0:T(8,128)} %bitcast.7, f32[64,128]{1,0:T(8,128)} %bitcast.11), custom_call_target="tpu_custom_call" | custom-call | tf_op jit(solution)/shard_map/pallas_call | solution.py:326
  91.9 1.3 %shard_map.87 = (f32[4,8,128]{2,1,0:T(8,128)}, f32[4,3]{1,0:T(4,128)}) custom-call(f32[4,8,128]{2,1,0:T(8,128)} %get-tuple-element.4.basis_ref, f32[8,128]{1,0:T(8,128)} %get-tuple-element.5.hess_ref), custom_call_target="tpu_custom_call" | custom-call | tf_op jit(solution)/shard_map/pallas_call | solution.py:359

commit v3 on v2

--- a/solution.py
+++ b/solution.py
@@ -22,9 +22,10 @@
     basis_ref, hess_ref,
     rv, av, fv, cf,
     near_c, near_a, c7, c9, c11, c12, c13,
+    n_own, n11, n12, n13, n_fin,
     xs, bs, gr,
     src1, src2, src3, srct, srcz, srcp,
-    h1, h2, h3, ht, hz, hp,
+    h1, h2, h3, ht, hm, hz, hp,
     lsem, msend, mrecv, rsend, rrecv,
 ):
     d = lax.axis_index("chain")
@@ -50,7 +51,7 @@
         load.start()
 
     partners = [dev(o) for o in (-12, -8, -4, -3, -2, -1, 1, 2, 3, 4, 8, 12)]
-    partners += [dev(16 * o) for o in range(1, 16)]
+    partners += [dev(16 * o + c) for o in range(1, 16) for c in (-1, 0, 1)]
     partners += [in_line(o) for o in range(1, 16)]
     barrier = pltpu.get_barrier_semaphore()
     for other in partners:
@@ -69,8 +70,11 @@
     for load in loads:
         load.wait()
 
-    send(rv, h1.at[0, 1], rsend.at[0, 0], rrecv.at[0, 0], dev(-1))
-    send(rv, h1.at[0, 0], rsend.at[0, 0], rrecv.at[0, 0], dev(1))
+    def pass_ends(j, src):
+        send(src, h1.at[j, 1], rsend.at[j, 0], rrecv.at[j, 0], dev(-1))
+        send(src, h1.at[j, 0], rsend.at[j, 0], rrecv.at[j, 0], dev(1))
+
+    pass_ends(0, rv)
     send(cf.at[pl.ds(0, 6)], near_c.at[1], msend.at[0], mrecv.at[0], dev(-1))
     send(cf.at[pl.ds(0, 6)], near_c.at[0], msend.at[0], mrecv.at[0], dev(1))
 
@@ -88,6 +92,10 @@
         for p in range(4, 16, 4):
             send(cf.at[12], c12.at[p // 4 - 1], msend.at[4], mrecv.at[4], dev(-16 * p))
         send(cf.at[13], c13, msend.at[5], mrecv.at[5], dev(-16 * 8))
+
+    def pass_on(k, src, dst):
+        send(src, dst.at[1], msend.at[k], mrecv.at[k], dev(-1))
+        send(src, dst.at[0], msend.at[k], mrecv.at[k], dev(1))
 
     def send_operator():
         send(av, near_a.at[1], msend.at[6], mrecv.at[6], dev(-1))
@@ -189,7 +197,7 @@
     xs[0, 2] = h1[0, 1] * has_above
     drain(near_c, mrecv.at[0])
 
-    def body(j, hess):
+    def body(j, hess, first=False):
         u = [xs[j, 0], xs[j, 1], xs[j, 2]]
         for level in range(NEAR):
             s = 2**level
@@ -210,7 +218,7 @@
             src[j] = x
             for k, o in enumerate(LOWS):
                 send(src.at[j], got.at[j, k], rsend.at[j, slot], rrecv.at[j, slot], dev(-o * by))
-            pl.when(j == 0)(later)
+            later()
             drain(got.at[j], rrecv.at[j, slot])
             f = {o: got[j, k] for k, o in enumerate(LOWS)}
             f[0] = x
@@ -222,56 +230,98 @@
             return far_level(cf.at[level + 1], y[0], y[-2], y[2], 0, 2 * by)
 
         def after_first():
-            send_low(False)
-            send_top()
-            drain(c7, mrecv.at[1])
+            if first:
+                send_low(False)
+                send_top()
+                drain(c7, mrecv.at[1])
+            else:
+                pl.when(j == 1)(lambda: pass_on(8, cf.at[pl.ds(11, 4)], n_own))
 
         def after_second():
-            send_operator()
-            drain(c9, mrecv.at[2])
+            if first:
+                send_operator()
+                drain(c9, mrecv.at[2])
+            else:
+
+                @pl.when(j == 1)
+                def _():
+                    pass_on(9, c12, n12)
+                    pass_on(10, c13, n13)
+                    pass_on(11, fv, n_fin)
 
         x = group(x, src2, h2, 1, c7, 7, 1, after_first)
         x = group(x, src3, h3, 2, c9, 9, 4, after_second)
 
         srct[j] = x
-        for o in range(1, 16):
-            send(srct.at[j], ht.at[j, o - 1], rsend.at[j, 3], rrecv.at[j, 3], dev(-16 * o))
+        slots = [(0, o) for o in range(1, 16)]
+        if not first:
+            slots += [(c, o) for c in (-1, 1) for o in range(16)]
+        got = ht if first else hm.at[j - 1]
+        for k, (c, o) in enumerate(slots):
+            send(srct.at[j], got.at[k], rsend.at[j, 3], rrecv.at[j, 3], dev(-16 * o - c))
         pass_sums(j)
 
-        @pl.when(j == 0)
-        def _():
+        if first:
             drain(c11, mrecv.at[3])
             drain(c12, mrecv.at[4])
             drain(c13, mrecv.at[5])
-
-        drain(ht.at[j], rrecv.at[j, 3])
-        f = [x] + [ht[j, o] for o in range(15)]
-
-        def top(coef, field, p, by):
-            return far_level(
-                coef, field[p], field[(p - by) % 16], field[(p + by) % 16], 16 * p, 16 * by
-            )
-
-        y1 = {p: top(cf.at[11] if p == 0 else c11.at[p // 2 - 1], f, p, 1) for p in range(0, 16, 2)}
-        y2 = {p: top(cf.at[12] if p == 0 else c12.at[p // 4 - 1], y1, p, 2) for p in range(0, 16, 4)}
-        y3 = {p: top(cf.at[13] if p == 0 else c13, y2, p, 4) for p in (0, 8)}
-        x = top(cf.at[14], y3, 0, 8)
-        x = x + mul(fv, x)
-
-        src1[j] = x
-        send(src1.at[j], h1.at[j + 1, 1], rsend.at[j + 1, 0], rrecv.at[j + 1, 0], dev(-1))
-        send(src1.at[j], h1.at[j + 1, 0], rsend.at[j + 1, 0], rrecv.at[j + 1, 0], dev(1))
+        else:
+
+            @pl.when(j == 1)
+            def _():
+                drain(n11, mrecv.at[7])
+                drain(n_own, mrecv.at[8])
+                drain(n12, mrecv.at[9])
+                drain(n13, mrecv.at[10])
+                drain(n_fin, mrecv.at[11])
+
+        drain(got, rrecv.at[j, 3])
+        fields = {(0, 0): x}
+        for k, key in enumerate(slots):
+            fields[key] = got[k]
+
+        def column(c):
+            if c == 0:
+                own, others, final = cf.at[pl.ds(11, 4)], (c11, c12, c13), fv
+            else:
+                side = max(c, 0)
+                own = n_own.at[side]
+                others, final = (n11.at[side], n12.at[side], n13.at[side]), n_fin.at[side]
+            y = [fields[c, o] for o in range(16)]
+            for rank in range(4):
+                by = 2**rank
+
+                def coef(p):
+                    if p == 0:
+                        return own.at[rank]
+                    return others[2] if rank == 2 else others[rank].at[p // (2 * by) - 1]
+
+                places = range(0, 16, 2 * by)
+                y = {
+                    p: far_level(
+                        coef(p), y[p], y[(p - by) % 16], y[(p + by) % 16], 16 * p + c, 16 * by
+                    )
+                    for p in places
+                }
+            return y[0] + mul(final, y[0])
+
+        x = column(0)
+        if first:
+            src1[...] = x
+            pass_ends(1, src1)
+            pass_on(7, c11, n11)
+        else:
+            sides = column(-1), column(1)
 
         h, inverse, new, hess = finish(j, xs[j, 1], hess)
         bs[j] = new
         basis_ref[j] = new
 
-        @pl.when(j == 0)
-        def _():
+        if first:
             drain(near_a, mrecv.at[6])
-
-        drain(h1.at[j + 1], rrecv.at[j + 1, 0])
-        cols = [h1[j + 1, 0] * has_below, x, h1[j + 1, 1] * has_above]
+            drain(h1.at[1], rrecv.at[1, 0])
+            sides = h1[1, 0], h1[1, 1]
+        cols = [sides[0] * has_below, x, sides[1] * has_above]
         for c, (coef, mask) in enumerate(
             ((near_a.at[0], has_below), (av, None), (near_a.at[1], has_above))
         ):
@@ -291,7 +341,8 @@
         send_sums(sums, j + 1)
         return hess
 
-    hess = lax.fori_loop(0, ITERS, body, zero)
+    hess = body(0, zero, True)
+    hess = lax.fori_loop(1, ITERS, body, hess)
     pass_sums(ITERS)
     _, _, new, hess = finish(ITERS, xs[ITERS, 1], hess)
     basis_ref[ITERS] = new
@@ -304,14 +355,17 @@
     drain(c12, msend.at[4])
     drain(c13, msend.at[5])
     drain(near_a, msend.at[6])
+    for k, buf in enumerate((n11, n_own, n12, n13, n_fin)):
+        drain(buf, msend.at[7 + k])
     for j in range(ITERS + 1):
-        drain(h1.at[j], rsend.at[j, 0])
         drain(hz.at[j, pl.ds(0, 15)], rsend.at[j, 4])
         drain(hp.at[j, pl.ds(0, 15)], rsend.at[j, 5])
+        if j < 2:
+            drain(h1.at[j], rsend.at[j, 0])
         if j < ITERS:
             drain(h2.at[j], rsend.at[j, 1])
             drain(h3.at[j], rsend.at[j, 2])
-            drain(ht.at[j], rsend.at[j, 3])
+            drain(ht if j == 0 else hm.at[j - 1], rsend.at[j, 3])
 
 
 def hand_out(basis_ref, hess_ref, basis_out, hess_out):
@@ -335,14 +389,16 @@
             vmem(*tile), vmem(3, *block), vmem(*block), vmem(15, 2, *block),
             vmem(2, 6, 2, *block), vmem(2, 3, *block), vmem(2, 2, *block), vmem(2, 2, *block),
             vmem(7, 2, *block), vmem(3, 2, *block), vmem(2, *block),
+            vmem(2, 4, 2, *block), vmem(2, 7, 2, *block), vmem(2, 3, 2, *block), vmem(2, 2, *block),
+            vmem(2, *block),
             vmem(4, 3, *tile), vmem(4, *tile), vmem(3, *tile),
-            vmem(3, *tile), vmem(3, *tile), vmem(3, *tile), vmem(3, *tile),
+            vmem(*tile), vmem(3, *tile), vmem(3, *tile), vmem(3, *tile),
             vmem(4, 1, ROWS), vmem(4, 1, ROWS),
-            vmem(4, 2, *tile), vmem(3, 6, *tile), vmem(3, 6, *tile), vmem(3, 15, *tile),
+            vmem(2, 2, *tile), vmem(3, 6, *tile), vmem(3, 6, *tile), vmem(15, *tile), vmem(2, 47, *tile),
             vmem(4, 16, ROWS), vmem(4, 16, ROWS),
             pltpu.SemaphoreType.DMA((7,)),
-            pltpu.SemaphoreType.DMA((7,)),
-            pltpu.SemaphoreType.DMA((7,)),
+            pltpu.SemaphoreType.DMA((12,)),
+            pltpu.SemaphoreType.DMA((12,)),
             pltpu.SemaphoreType.DMA((4, 6)),
             pltpu.SemaphoreType.DMA((4, 6)),
         ],

time: 93.4 us -> 92.2 us (0.987)
  Pallas kernels: 92.6 us -> 91.4 us
    pallas_call x1, Pallas kernels: 91.2 us -> 90.1 us  [on_device(): pl.pallas_call(kernel, out_shape=(jax.ShapeDtypeStruct((ITERS + 1, 8, ROW...]
where the time goes in v3:
time: 92.2 us; the launch traced here: 92 us
  Pallas kernels  91.4 us (99%)
    pallas_call x1, Pallas kernels, on_device(): pl.pallas_call(kernel, out_shape=(jax.ShapeDtypeStruct((ITERS + 1, 8, ROW...  90.1 us

profile of v3, /device:TPU:1, one launch (start us, length us, event | category | flops | bytes accessed | tf_op | source)
XLA Modules:
  0.0 92.0 jit_solution(2591854781052217760)
XLA Ops:
  0.6 90.1 %shard_map.86 = (f32[4,8,128]{2,1,0:T(8,128)}, f32[8,128]{1,0:T(8,128)}) custom-call(f32[8,128]{1,0:T(8,128)} %r_hbm.1, f32[64,128]{1,0:T(8,128)} %bitcast.8, f32[64,128]{1,0:T(8,128)} %bitcast.9, f32[64,128]{1,0:T(8,128)} %bitcast.10, f32[15,64,128]{2,1,0:T(8,128)} %bitcast.6, f32[15,64,128]{2,1,0:T(8,128)} %bitcast.7, f32[64,128]{1,0:T(8,128)} %bitcast.11), custom_call_target="tpu_custom_call" | custom-call | tf_op jit(solution)/shard_map/pallas_call | solution.py:380
  90.7 1.3 %shard_map.87 = (f32[4,8,128]{2,1,0:T(8,128)}, f32[4,3]{1,0:T(4,128)}) custom-call(f32[4,8,128]{2,1,0:T(8,128)} %get-tuple-element.4.basis_ref, f32[8,128]{1,0:T(8,128)} %get-tuple-element.5.hess_ref), custom_call_target="tpu_custom_call" | custom-call | tf_op jit(solution)/shard_map/pallas_call | solution.py:415

commit v4 on v2

--- a/solution.py
+++ b/solution.py
@@ -21,7 +21,7 @@
     r_hbm, dg_hbm, bl_hbm, ab_hbm, lo_hbm, up_hbm, fb_hbm,
     basis_ref, hess_ref,
     rv, av, fv, cf,
-    near_c, near_a, c7, c9, c11, c12, c13,
+    packs, got_packs, near_c, near_a, c7, c9, c11, c12, c13,
     xs, bs, gr,
     src1, src2, src3, srct, srcz, srcp,
     h1, h2, h3, ht, hz, hp,
@@ -55,7 +55,6 @@
     barrier = pltpu.get_barrier_semaphore()
     for other in partners:
         pl.semaphore_signal(barrier, inc=1, device_id=(other,), device_id_type=pl.DeviceIdType.MESH)
-    pl.semaphore_wait(barrier, len(partners))
 
     def send(src, dst, ssem, rsem, other):
         pltpu.make_async_remote_copy(
@@ -68,11 +67,6 @@
 
     for load in loads:
         load.wait()
-
-    send(rv, h1.at[0, 1], rsend.at[0, 0], rrecv.at[0, 0], dev(-1))
-    send(rv, h1.at[0, 0], rsend.at[0, 0], rrecv.at[0, 0], dev(1))
-    send(cf.at[pl.ds(0, 6)], near_c.at[1], msend.at[0], mrecv.at[0], dev(-1))
-    send(cf.at[pl.ds(0, 6)], near_c.at[0], msend.at[0], mrecv.at[0], dev(1))
 
     def send_low(first):
         if first:
@@ -88,12 +82,6 @@
         for p in range(4, 16, 4):
             send(cf.at[12], c12.at[p // 4 - 1], msend.at[4], mrecv.at[4], dev(-16 * p))
         send(cf.at[13], c13, msend.at[5], mrecv.at[5], dev(-16 * 8))
-
-    def send_operator():
-        send(av, near_a.at[1], msend.at[6], mrecv.at[6], dev(-1))
-        send(av, near_a.at[0], msend.at[6], mrecv.at[6], dev(1))
-
-    send_low(True)
 
     lane = lax.broadcasted_iota(jnp.int32, (8, ROWS), 1)
     sub = lax.broadcasted_iota(jnp.int32, (8, ROWS), 0)
@@ -172,6 +160,21 @@
         hess = jnp.where(lane == j - 1, column, hess)
         return h, inverse, new, hess
 
+    def make_strips(j, f, w):
+        low, high, v = f, f, w
+        for level in range(NEAR - 1):
+            s = 2**level
+            low = jnp.where(lane >= 2 * s, pltpu.roll(v, s, 1), low)
+            high = jnp.where(lane < ROWS - 2 * s, pltpu.roll(v, ROWS - s, 1), high)
+            if level < NEAR - 2:
+                v = step(cf.at[level], v, pltpu.roll(v, s, 1), pltpu.roll(v, ROWS - s, 1))
+        src1[j, 0] = low
+        src1[j, 1] = high
+
+    def ship_strips(j):
+        send(src1.at[j, 0], h1.at[j, 1], rsend.at[j, 0], rrecv.at[j, 0], dev(-1))
+        send(src1.at[j, 1], h1.at[j, 0], rsend.at[j, 0], rrecv.at[j, 0], dev(1))
+
     zero = jnp.zeros((8, ROWS), F32)
     for i in range(4):
         bs[i] = zero
@@ -182,15 +185,49 @@
             xs[i, c] = zero
 
     r = rv[...]
+    make_strips(0, r, r)
+    wide = lax.broadcasted_iota(jnp.int32, (64, ROWS), 1)
+
+    for which in range(2):
+        low = jnp.where(wide < 1, av[1 + which], pltpu.roll(av[0], 1, 1))
+        high = jnp.where(wide >= ROWS - 1, av[1 + which], pltpu.roll(av[0], ROWS - 1, 1))
+        for level in range(NEAR - 1):
+            w = 2 ** (level + 1)
+            low = jnp.where(wide >= w, pltpu.roll(cf[level, which], w, 1), low)
+            high = jnp.where(wide < ROWS - w, pltpu.roll(cf[level, which], ROWS - w, 1), high)
+        packs[0, which] = low
+        packs[1, which] = high
+    pl.semaphore_wait(barrier, len(partners))
+    ship_strips(0)
+    send(packs.at[0], got_packs.at[1], msend.at[0], mrecv.at[0], dev(-1))
+    send(packs.at[1], got_packs.at[0], msend.at[0], mrecv.at[0], dev(1))
+    send_low(True)
     send_sums(jnp.where(sub == 3, jnp.sum(r * r, axis=0, keepdims=True) + zero, 0.0), 0)
     drain(h1.at[0], rrecv.at[0, 0])
     xs[0, 0] = h1[0, 0] * has_below
     xs[0, 1] = r
     xs[0, 2] = h1[0, 1] * has_above
-    drain(near_c, mrecv.at[0])
+    drain(got_packs, mrecv.at[0])
+    for side in range(2):
+        for which in range(2):
+            pack = got_packs[side, which]
+            near_a[side, 1 + which] = pack
+            for level in range(NEAR - 1):
+                w = 2 ** (level + 1)
+                near_c[side, level, which] = pltpu.roll(pack, w if side == 0 else ROWS - w, 1)
+        near_a[side, 0] = pltpu.roll(got_packs[side, 0], 1 if side == 0 else ROWS - 1, 1)
 
     def body(j, hess):
-        u = [xs[j, 0], xs[j, 1], xs[j, 2]]
+        strip = [h1[j, 0] * has_below, h1[j, 1] * has_above]
+
+        def join(left, right, k):
+            return (
+                jnp.where(lane >= ROWS - k, left, pltpu.roll(strip[0], k, 1)),
+                jnp.where(lane < k, right, pltpu.roll(strip[1], ROWS - k, 1)),
+            )
+
+        left, right = join(xs[j, 0], xs[j, 2], 1)
+        u = [left, xs[j, 1], right]
         for level in range(NEAR):
             s = 2**level
             mid = step(cf.at[level], u[1], down(u[1], u[0], s), upward(u[1], u[2], s))
@@ -201,6 +238,8 @@
                 right = step(
                     near_c.at[1, level], u[2], down(u[2], u[1], s), upward(u[2], u[2], s)
                 ) * has_above
+                if level < NEAR - 2:
+                    left, right = join(left, right, 2 * s)
                 u = [left, mid, right]
             else:
                 u = [None, mid, None]
@@ -227,7 +266,6 @@
             drain(c7, mrecv.at[1])
 
         def after_second():
-            send_operator()
             drain(c9, mrecv.at[2])
 
         x = group(x, src2, h2, 1, c7, 7, 1, after_first)
@@ -258,30 +296,26 @@
         x = top(cf.at[14], y3, 0, 8)
         x = x + mul(fv, x)
 
-        src1[j] = x
-        send(src1.at[j], h1.at[j + 1, 1], rsend.at[j + 1, 0], rrecv.at[j + 1, 0], dev(-1))
-        send(src1.at[j], h1.at[j + 1, 0], rsend.at[j + 1, 0], rrecv.at[j + 1, 0], dev(1))
-
         h, inverse, new, hess = finish(j, xs[j, 1], hess)
         bs[j] = new
         basis_ref[j] = new
 
-        @pl.when(j == 0)
-        def _():
-            drain(near_a, mrecv.at[6])
-
-        drain(h1.at[j + 1], rrecv.at[j + 1, 0])
-        cols = [h1[j + 1, 0] * has_below, x, h1[j + 1, 1] * has_above]
-        for c, (coef, mask) in enumerate(
-            ((near_a.at[0], has_below), (av, None), (near_a.at[1], has_above))
-        ):
-            v = 2.0 * cols[c] + mul(coef.at[0], cols[c])
-            v = v + mul(coef.at[1], down(cols[c], cols[max(c - 1, 0)], 1))
-            v = v + mul(coef.at[2], upward(cols[c], cols[min(c + 1, 2)], 1))
+        def operate(coef, c, f, below, above):
+            v = 2.0 * f + mul(coef.at[0], f) + mul(coef.at[1], below) + mul(coef.at[2], above)
             for i in range(2):
                 v = v - h[i] * xs[i + 1, c]
-            v = v * inverse
-            xs[j + 1, c] = v if mask is None else v * mask
+            return v * inverse
+
+        make_strips(j + 1, x, operate(av, 1, x, pltpu.roll(x, 1, 1), pltpu.roll(x, ROWS - 1, 1)))
+        ship_strips(j + 1)
+        drain(h1.at[j + 1], rrecv.at[j + 1, 0])
+        left, right = h1[j + 1, 0] * has_below, h1[j + 1, 1] * has_above
+        middle = operate(av, 1, x, down(x, left, 1), upward(x, right, 1))
+        left = operate(near_a.at[0], 0, left, down(left, left, 1), upward(left, x, 1))
+        right = operate(near_a.at[1], 2, right, down(right, x, 1), upward(right, right, 1))
+        xs[j + 1, 0] = left * has_below
+        xs[j + 1, 1] = middle
+        xs[j + 1, 2] = right * has_above
 
         w = xs[j + 1, 1]
         sums = zero
@@ -297,13 +331,12 @@
     basis_ref[ITERS] = new
     hess_ref[...] = hess
 
-    drain(near_c, msend.at[0])
+    drain(packs, msend.at[0])
     drain(c7, msend.at[1])
     drain(c9, msend.at[2])
     drain(c11, msend.at[3])
     drain(c12, msend.at[4])
     drain(c13, msend.at[5])
-    drain(near_a, msend.at[6])
     for j in range(ITERS + 1):
         drain(h1.at[j], rsend.at[j, 0])
         drain(hz.at[j, pl.ds(0, 15)], rsend.at[j, 4])
@@ -333,10 +366,10 @@
         out_specs=(pl.BlockSpec(memory_space=pltpu.VMEM), pl.BlockSpec(memory_space=pltpu.VMEM)),
         scratch_shapes=[
             vmem(*tile), vmem(3, *block), vmem(*block), vmem(15, 2, *block),
-            vmem(2, 6, 2, *block), vmem(2, 3, *block), vmem(2, 2, *block), vmem(2, 2, *block),
+            vmem(2, 2, *block), vmem(2, 2, *block), vmem(2, 6, 2, *block), vmem(2, 3, *block), vmem(2, 2, *block), vmem(2, 2, *block),
             vmem(7, 2, *block), vmem(3, 2, *block), vmem(2, *block),
             vmem(4, 3, *tile), vmem(4, *tile), vmem(3, *tile),
-            vmem(3, *tile), vmem(3, *tile), vmem(3, *tile), vmem(3, *tile),
+            vmem(4, 2, *tile), vmem(3, *tile), vmem(3, *tile), vmem(3, *tile),
             vmem(4, 1, ROWS), vmem(4, 1, ROWS),
             vmem(4, 2, *tile), vmem(3, 6, *tile), vmem(3, 6, *tile), vmem(3, 15, *tile),
             vmem(4, 16, ROWS), vmem(4, 16, ROWS),

time: 93.4 us -> 91.9 us (0.984)
  Pallas kernels: 92.6 us -> 91.1 us
    pallas_call x1, Pallas kernels: 91.2 us -> 89.7 us  [on_device(): pl.pallas_call(kernel, out_shape=(jax.ShapeDtypeStruct((ITERS + 1, 8, ROW...]
where the time goes in v4:
time: 91.9 us; the launch traced here: 91.7 us
  Pallas kernels  91.1 us (99%)
    pallas_call x1, Pallas kernels, on_device(): pl.pallas_call(kernel, out_shape=(jax.ShapeDtypeStruct((ITERS + 1, 8, ROW...  89.7 us

profile of v4, /device:TPU:1, one launch (start us, length us, event | category | flops | bytes accessed | tf_op | source)
XLA Modules:
  0.0 91.7 jit_solution(15042500554319156021)
XLA Ops:
  0.6 89.7 %shard_map.86 = (f32[4,8,128]{2,1,0:T(8,128)}, f32[8,128]{1,0:T(8,128)}) custom-call(f32[8,128]{1,0:T(8,128)} %r_hbm.1, f32[64,128]{1,0:T(8,128)} %bitcast.8, f32[64,128]{1,0:T(8,128)} %bitcast.9, f32[64,128]{1,0:T(8,128)} %bitcast.10, f32[15,64,128]{2,1,0:T(8,128)} %bitcast.6, f32[15,64,128]{2,1,0:T(8,128)} %bitcast.7, f32[64,128]{1,0:T(8,128)} %bitcast.11), custom_call_target="tpu_custom_call" | custom-call | tf_op jit(solution)/shard_map/pallas_call | solution.py:359
  90.4 1.3 %shard_map.87 = (f32[4,8,128]{2,1,0:T(8,128)}, f32[4,3]{1,0:T(4,128)}) custom-call(f32[4,8,128]{2,1,0:T(8,128)} %get-tuple-element.4.basis_ref, f32[8,128]{1,0:T(8,128)} %get-tuple-element.5.hess_ref), custom_call_target="tpu_custom_call" | custom-call | tf_op jit(solution)/shard_map/pallas_call | solution.py:392

commit v5 on v4

--- a/solution.py
+++ b/solution.py
@@ -22,9 +22,10 @@
     basis_ref, hess_ref,
     rv, av, fv, cf,
     packs, got_packs, near_c, near_a, c7, c9, c11, c12, c13,
+    edges, got_edges, edge_c, edge_f,
     xs, bs, gr,
     src1, src2, src3, srct, srcz, srcp,
-    h1, h2, h3, ht, hz, hp,
+    h1, h2, h3, ht, hm, hz, hp,
     lsem, msend, mrecv, rsend, rrecv,
 ):
     d = lax.axis_index("chain")
@@ -50,7 +51,7 @@
         load.start()
 
     partners = [dev(o) for o in (-12, -8, -4, -3, -2, -1, 1, 2, 3, 4, 8, 12)]
-    partners += [dev(16 * o) for o in range(1, 16)]
+    partners += [dev(16 * o + c) for o in range(1, 16) for c in (-1, 0, 1)]
     partners += [in_line(o) for o in range(1, 16)]
     barrier = pltpu.get_barrier_semaphore()
     for other in partners:
@@ -217,7 +218,72 @@
                 near_c[side, level, which] = pltpu.roll(pack, w if side == 0 else ROWS - w, 1)
         near_a[side, 0] = pltpu.roll(got_packs[side, 0], 1 if side == 0 else ROWS - 1, 1)
 
-    def body(j, hess):
+    def top_blocks():
+        yield 0, 0, cf.at[11]
+        yield 1, 0, cf.at[12]
+        yield 2, 0, cf.at[13]
+        yield 3, 0, cf.at[14]
+        yield 2, 8, c13
+        for p in range(2, 16, 2):
+            yield 0, p, c11.at[p // 2 - 1]
+        for p in range(4, 16, 4):
+            yield 1, p, c12.at[p // 4 - 1]
+
+    def send_edges():
+        for side, row in ((0, 0), (1, ROWS - 1)):
+            pack = jnp.where(wide == 33, pltpu.roll(fv[...], (33 - row) % ROWS, 1), 0.0)
+            for rank, p, blocks in top_blocks():
+                for which in range(2):
+                    to = 16 * (2 * rank + which) + p
+                    pack = jnp.where(
+                        wide == to, pltpu.roll(blocks[which], (to - row) % ROWS, 1), pack
+                    )
+            edges[side] = pack
+        send(edges.at[0], got_edges.at[1], msend.at[6], mrecv.at[6], dev(-1))
+        send(edges.at[1], got_edges.at[0], msend.at[6], mrecv.at[6], dev(1))
+
+    def spread(v, index):
+        v = jnp.where(index < 16, v, 0.0)
+        v = v + pltpu.roll(v, 16, 1)
+        v = v + pltpu.roll(v, 32, 1)
+        return v + pltpu.roll(v, 64, 1)
+
+    def take_edges():
+        drain(got_edges, mrecv.at[6])
+        for side in range(2):
+            pack = got_edges[side]
+            edge_f[side] = pltpu.roll(pack, ROWS - 33, 1)
+            for rank in range(4):
+                for which in range(2):
+                    start = 16 * (2 * rank + which)
+                    part = pltpu.roll(pack, ROWS - start, 1) if start else pack
+                    edge_c[side, rank, which] = spread(part, wide)
+
+    def edge(side, fields):
+        row, c = ((ROWS - 1, -1), (0, 1))[side]
+        y = zero
+        for p in range(16):
+            moved = pltpu.roll(fields[p], (p - row) % ROWS, 1) if p != row else fields[p]
+            y = jnp.where(lane == p, moved, y)
+        y = spread(y, lane)
+        place = lax.rem(d + (c % DEV) + 16 * lax.rem(lane, 16), DEV)
+        for rank in range(4):
+            by = 2**rank
+            below = jnp.where(place >= 16 * by, pltpu.roll(y, by, 1), 0.0)
+            above = jnp.where(place + 16 * by <= DEV - 1, pltpu.roll(y, ROWS - by, 1), 0.0)
+            y = step(edge_c.at[side, rank], y, below, above)
+        return y + mul(edge_f.at[side], y)
+
+    def finish_sums(j, new, hess):
+        w = xs[j + 1, 1]
+        sums = zero
+        rows = [bs[0] * w, bs[1] * w, bs[2] * w, w * w, bs[0] * new, bs[1] * new, bs[2] * new]
+        for i, row in enumerate(rows):
+            sums = jnp.where(sub == i, jnp.sum(row, axis=0, keepdims=True) + zero, sums)
+        send_sums(sums, j + 1)
+        return hess
+
+    def body(j, hess, last=False):
         strip = [h1[j, 0] * has_below, h1[j, 1] * has_above]
 
         def join(left, right, k):
@@ -249,7 +315,7 @@
             src[j] = x
             for k, o in enumerate(LOWS):
                 send(src.at[j], got.at[j, k], rsend.at[j, slot], rrecv.at[j, slot], dev(-o * by))
-            pl.when(j == 0)(later)
+            later()
             drain(got.at[j], rrecv.at[j, slot])
             f = {o: got[j, k] for k, o in enumerate(LOWS)}
             f[0] = x
@@ -261,29 +327,45 @@
             return far_level(cf.at[level + 1], y[0], y[-2], y[2], 0, 2 * by)
 
         def after_first():
-            send_low(False)
-            send_top()
-            drain(c7, mrecv.at[1])
+            if not last:
+
+                @pl.when(j == 0)
+                def _():
+                    send_low(False)
+                    send_top()
+                    drain(c7, mrecv.at[1])
 
         def after_second():
-            drain(c9, mrecv.at[2])
+            if not last:
+
+                @pl.when(j == 0)
+                def _():
+                    drain(c9, mrecv.at[2])
+
+                pl.when(j == 1)(take_edges)
 
         x = group(x, src2, h2, 1, c7, 7, 1, after_first)
         x = group(x, src3, h3, 2, c9, 9, 4, after_second)
 
         srct[j] = x
-        for o in range(1, 16):
-            send(srct.at[j], ht.at[j, o - 1], rsend.at[j, 3], rrecv.at[j, 3], dev(-16 * o))
+        slots = [(0, o) for o in range(1, 16)]
+        if last:
+            slots += [(c, o) for c in (-1, 1) for o in range(16)]
+        got = hm if last else ht.at[j]
+        for k, (c, o) in enumerate(slots):
+            send(srct.at[j], got.at[k], rsend.at[j, 3], rrecv.at[j, 3], dev(-16 * o - c))
         pass_sums(j)
 
-        @pl.when(j == 0)
-        def _():
-            drain(c11, mrecv.at[3])
-            drain(c12, mrecv.at[4])
-            drain(c13, mrecv.at[5])
-
-        drain(ht.at[j], rrecv.at[j, 3])
-        f = [x] + [ht[j, o] for o in range(15)]
+        if not last:
+
+            @pl.when(j == 0)
+            def _():
+                drain(c11, mrecv.at[3])
+                drain(c12, mrecv.at[4])
+                drain(c13, mrecv.at[5])
+
+        drain(got, rrecv.at[j, 3])
+        f = [x] + [got[o] for o in range(15)]
 
         def top(coef, field, p, by):
             return far_level(
@@ -306,8 +388,16 @@
                 v = v - h[i] * xs[i + 1, c]
             return v * inverse
 
+        if last:
+            left = edge(0, [got[15 + o] for o in range(16)])
+            left = pltpu.roll(left, ROWS - 1, 1) * has_below
+            right = edge(1, [got[31 + o] for o in range(16)]) * has_above
+            xs[j + 1, 1] = operate(av, 1, x, down(x, left, 1), upward(x, right, 1))
+            return finish_sums(j, new, hess)
+
         make_strips(j + 1, x, operate(av, 1, x, pltpu.roll(x, 1, 1), pltpu.roll(x, ROWS - 1, 1)))
         ship_strips(j + 1)
+        pl.when(j == 0)(send_edges)
         drain(h1.at[j + 1], rrecv.at[j + 1, 0])
         left, right = h1[j + 1, 0] * has_below, h1[j + 1, 1] * has_above
         middle = operate(av, 1, x, down(x, left, 1), upward(x, right, 1))
@@ -317,34 +407,30 @@
         xs[j + 1, 1] = middle
         xs[j + 1, 2] = right * has_above
 
-        w = xs[j + 1, 1]
-        sums = zero
-        rows = [bs[0] * w, bs[1] * w, bs[2] * w, w * w, bs[0] * new, bs[1] * new, bs[2] * new]
-        for i, row in enumerate(rows):
-            sums = jnp.where(sub == i, jnp.sum(row, axis=0, keepdims=True) + zero, sums)
-        send_sums(sums, j + 1)
-        return hess
-
-    hess = lax.fori_loop(0, ITERS, body, zero)
+        return finish_sums(j, new, hess)
+
+    hess = lax.fori_loop(0, ITERS - 1, body, zero)
+    hess = body(ITERS - 1, hess, True)
     pass_sums(ITERS)
     _, _, new, hess = finish(ITERS, xs[ITERS, 1], hess)
     basis_ref[ITERS] = new
     hess_ref[...] = hess
 
     drain(packs, msend.at[0])
+    drain(edges, msend.at[6])
     drain(c7, msend.at[1])
     drain(c9, msend.at[2])
     drain(c11, msend.at[3])
     drain(c12, msend.at[4])
     drain(c13, msend.at[5])
     for j in range(ITERS + 1):
-        drain(h1.at[j], rsend.at[j, 0])
         drain(hz.at[j, pl.ds(0, 15)], rsend.at[j, 4])
         drain(hp.at[j, pl.ds(0, 15)], rsend.at[j, 5])
         if j < ITERS:
+            drain(h1.at[j], rsend.at[j, 0])
             drain(h2.at[j], rsend.at[j, 1])
             drain(h3.at[j], rsend.at[j, 2])
-            drain(ht.at[j], rsend.at[j, 3])
+            drain(ht.at[j] if j < 2 else hm, rsend.at[j, 3])
 
 
 def hand_out(basis_ref, hess_ref, basis_out, hess_out):
@@ -368,10 +454,11 @@
             vmem(*tile), vmem(3, *block), vmem(*block), vmem(15, 2, *block),
             vmem(2, 2, *block), vmem(2, 2, *block), vmem(2, 6, 2, *block), vmem(2, 3, *block), vmem(2, 2, *block), vmem(2, 2, *block),
             vmem(7, 2, *block), vmem(3, 2, *block), vmem(2, *block),
+            vmem(2, *block), vmem(2, *block), vmem(2, 4, 2, *block), vmem(2, *block),
             vmem(4, 3, *tile), vmem(4, *tile), vmem(3, *tile),
             vmem(4, 2, *tile), vmem(3, *tile), vmem(3, *tile), vmem(3, *tile),
             vmem(4, 1, ROWS), vmem(4, 1, ROWS),
-            vmem(4, 2, *tile), vmem(3, 6, *tile), vmem(3, 6, *tile), vmem(3, 15, *tile),
+            vmem(3, 2, *tile), vmem(3, 6, *tile), vmem(3, 6, *tile), vmem(2, 15, *tile), vmem(47, *tile),
             vmem(4, 16, ROWS), vmem(4, 16, ROWS),
             pltpu.SemaphoreType.DMA((7,)),
             pltpu.SemaphoreType.DMA((7,)),

time: 91.9 us -> 90.9 us (0.989)
  Pallas kernels: 91.1 us -> 90.1 us
    pallas_call x1, Pallas kernels: 89.7 us -> 88.8 us  [on_device(): pl.pallas_call(kernel, out_shape=(jax.ShapeDtypeStruct((ITERS + 1, 8, ROW...]
where the time goes in v5:
time: 90.9 us; the launch traced here: 90.7 us
  Pallas kernels  90.1 us (99%)
    pallas_call x1, Pallas kernels, on_device(): pl.pallas_call(kernel, out_shape=(jax.ShapeDtypeStruct((ITERS + 1, 8, ROW...  88.8 us

profile of v5, /device:TPU:1, one launch (start us, length us, event | category | flops | bytes accessed | tf_op | source)
XLA Modules:
  0.0 90.7 jit_solution(16955823700009475708)
XLA Ops:
  0.6 88.8 %shard_map.86 = (f32[4,8,128]{2,1,0:T(8,128)}, f32[8,128]{1,0:T(8,128)}) custom-call(f32[8,128]{1,0:T(8,128)} %r_hbm.1, f32[64,128]{1,0:T(8,128)} %bitcast.8, f32[64,128]{1,0:T(8,128)} %bitcast.9, f32[64,128]{1,0:T(8,128)} %bitcast.10, f32[15,64,128]{2,1,0:T(8,128)} %bitcast.6, f32[15,64,128]{2,1,0:T(8,128)} %bitcast.7, f32[64,128]{1,0:T(8,128)} %bitcast.11), custom_call_target="tpu_custom_call" | custom-call | tf_op jit(solution)/shard_map/pallas_call | solution.py:445
  89.4 1.3 %shard_map.87 = (f32[4,8,128]{2,1,0:T(8,128)}, f32[4,3]{1,0:T(4,128)}) custom-call(f32[4,8,128]{2,1,0:T(8,128)} %get-tuple-element.4.basis_ref, f32[8,128]{1,0:T(8,128)} %get-tuple-element.5.hess_ref), custom_call_target="tpu_custom_call" | custom-call | tf_op jit(solution)/shard_map/pallas_call | solution.py:479

commit v6 on v5

--- a/solution.py
+++ b/solution.py
@@ -40,12 +40,14 @@
 
     loads = [
         pltpu.make_async_copy(r_hbm, rv, lsem.at[0]),
-        pltpu.make_async_copy(lo_hbm, cf.at[:, 0], lsem.at[1]),
-        pltpu.make_async_copy(up_hbm, cf.at[:, 1], lsem.at[2]),
+        pltpu.make_async_copy(lo_hbm.at[pl.ds(0, 8)], cf.at[pl.ds(0, 8), 0], lsem.at[1]),
+        pltpu.make_async_copy(up_hbm.at[pl.ds(0, 8)], cf.at[pl.ds(0, 8), 1], lsem.at[2]),
         pltpu.make_async_copy(dg_hbm, av.at[0], lsem.at[3]),
         pltpu.make_async_copy(bl_hbm, av.at[1], lsem.at[4]),
         pltpu.make_async_copy(ab_hbm, av.at[2], lsem.at[5]),
         pltpu.make_async_copy(fb_hbm, fv, lsem.at[6]),
+        pltpu.make_async_copy(lo_hbm.at[pl.ds(8, 7)], cf.at[pl.ds(8, 7), 0], lsem.at[7]),
+        pltpu.make_async_copy(up_hbm.at[pl.ds(8, 7)], cf.at[pl.ds(8, 7), 1], lsem.at[8]),
     ]
     for load in loads:
         load.start()
@@ -66,7 +68,7 @@
     def drain(buf, sem):
         pltpu.make_async_copy(buf, buf, sem).wait()
 
-    for load in loads:
+    for load in loads[:6]:
         load.wait()
 
     def send_low(first):
@@ -186,7 +188,6 @@
             xs[i, c] = zero
 
     r = rv[...]
-    make_strips(0, r, r)
     wide = lax.broadcasted_iota(jnp.int32, (64, ROWS), 1)
 
     for which in range(2):
@@ -199,11 +200,14 @@
         packs[0, which] = low
         packs[1, which] = high
     pl.semaphore_wait(barrier, len(partners))
-    ship_strips(0)
     send(packs.at[0], got_packs.at[1], msend.at[0], mrecv.at[0], dev(-1))
     send(packs.at[1], got_packs.at[0], msend.at[0], mrecv.at[0], dev(1))
+    make_strips(0, r, r)
+    ship_strips(0)
     send_low(True)
     send_sums(jnp.where(sub == 3, jnp.sum(r * r, axis=0, keepdims=True) + zero, 0.0), 0)
+    for load in loads[6:]:
+        load.wait()
     drain(h1.at[0], rrecv.at[0, 0])
     xs[0, 0] = h1[0, 0] * has_below
     xs[0, 1] = r
@@ -336,6 +340,7 @@
                     drain(c7, mrecv.at[1])
 
         def after_second():
+            pass_sums(j)
             if not last:
 
                 @pl.when(j == 0)
@@ -354,7 +359,9 @@
         got = hm if last else ht.at[j]
         for k, (c, o) in enumerate(slots):
             send(srct.at[j], got.at[k], rsend.at[j, 3], rrecv.at[j, 3], dev(-16 * o - c))
-        pass_sums(j)
+        h, inverse, new, hess = finish(j, xs[j, 1], hess)
+        bs[j] = new
+        basis_ref[j] = new
 
         if not last:
 
@@ -377,10 +384,6 @@
         y3 = {p: top(cf.at[13] if p == 0 else c13, y2, p, 4) for p in (0, 8)}
         x = top(cf.at[14], y3, 0, 8)
         x = x + mul(fv, x)
-
-        h, inverse, new, hess = finish(j, xs[j, 1], hess)
-        bs[j] = new
-        basis_ref[j] = new
 
         def operate(coef, c, f, below, above):
             v = 2.0 * f + mul(coef.at[0], f) + mul(coef.at[1], below) + mul(coef.at[2], above)
@@ -460,7 +463,7 @@
             vmem(4, 1, ROWS), vmem(4, 1, ROWS),
             vmem(3, 2, *tile), vmem(3, 6, *tile), vmem(3, 6, *tile), vmem(2, 15, *tile), vmem(47, *tile),
             vmem(4, 16, ROWS), vmem(4, 16, ROWS),
-            pltpu.SemaphoreType.DMA((7,)),
+            pltpu.SemaphoreType.DMA((9,)),
             pltpu.SemaphoreType.DMA((7,)),
             pltpu.SemaphoreType.DMA((7,)),
             pltpu.SemaphoreType.DMA((4, 6)),

time: 90.9 us -> 92.1 us (1.013)
  Pallas kernels: 90.1 us -> 91.2 us
    pallas_call x1, Pallas kernels: 88.8 us -> 89.9 us  [on_device(): pl.pallas_call(kernel, out_shape=(jax.ShapeDtypeStruct((ITERS + 1, 8, ROW...]
where the time goes in v6:
time: 92.1 us; the launch traced here: 91.9 us
  Pallas kernels  91.2 us (99%)
    pallas_call x1, Pallas kernels, on_device(): pl.pallas_call(kernel, out_shape=(jax.ShapeDtypeStruct((ITERS + 1, 8, ROW...  89.9 us

profile of v6, /device:TPU:1, one launch (start us, length us, event | category | flops | bytes accessed | tf_op | source)
XLA Modules:
  0.0 91.9 jit_solution(11267316646291698346)
XLA Ops:
  0.6 89.9 %shard_map.86 = (f32[4,8,128]{2,1,0:T(8,128)}, f32[8,128]{1,0:T(8,128)}) custom-call(f32[8,128]{1,0:T(8,128)} %r_hbm.1, f32[64,128]{1,0:T(8,128)} %bitcast.8, f32[64,128]{1,0:T(8,128)} %bitcast.9, f32[64,128]{1,0:T(8,128)} %bitcast.10, f32[15,64,128]{2,1,0:T(8,128)} %bitcast.6, f32[15,64,128]{2,1,0:T(8,128)} %bitcast.7, f32[64,128]{1,0:T(8,128)} %bitcast.11), custom_call_target="tpu_custom_call" | custom-call | tf_op jit(solution)/shard_map/pallas_call | solution.py:448
  90.5 1.3 %shard_map.87 = (f32[4,8,128]{2,1,0:T(8,128)}, f32[4,3]{1,0:T(4,128)}) custom-call(f32[4,8,128]{2,1,0:T(8,128)} %get-tuple-element.4.basis_ref, f32[8,128]{1,0:T(8,128)} %get-tuple-element.5.hess_ref), custom_call_target="tpu_custom_call" | custom-call | tf_op jit(solution)/shard_map/pallas_call | solution.py:482

commit v7 on v5

--- a/solution.py
+++ b/solution.py
@@ -21,7 +21,7 @@
     r_hbm, dg_hbm, bl_hbm, ab_hbm, lo_hbm, up_hbm, fb_hbm,
     basis_ref, hess_ref,
     rv, av, fv, cf,
-    packs, got_packs, near_c, near_a, c7, c9, c11, c12, c13,
+    packs, got_packs, triangle, near_c, near_a, c7, c9, c11, c12, c13,
     edges, got_edges, edge_c, edge_f,
     xs, bs, gr,
     src1, src2, src3, srct, srcz, srcp,
@@ -76,6 +76,14 @@
         else:
             send(cf.at[9], c9.at[1], msend.at[2], mrecv.at[2], dev(-8))
             send(cf.at[9], c9.at[0], msend.at[2], mrecv.at[2], dev(8))
+
+    def send_near():
+        send(cf.at[pl.ds(0, 6)], near_c.at[1], msend.at[7], mrecv.at[7], dev(-1))
+        send(cf.at[pl.ds(0, 6)], near_c.at[0], msend.at[7], mrecv.at[7], dev(1))
+
+    def send_operator():
+        send(av, near_a.at[1], msend.at[8], mrecv.at[8], dev(-1))
+        send(av, near_a.at[0], msend.at[8], mrecv.at[8], dev(1))
 
     def send_top():
         for p in range(2, 16, 2):
@@ -190,8 +198,7 @@
     wide = lax.broadcasted_iota(jnp.int32, (64, ROWS), 1)
 
     for which in range(2):
-        low = jnp.where(wide < 1, av[1 + which], pltpu.roll(av[0], 1, 1))
-        high = jnp.where(wide >= ROWS - 1, av[1 + which], pltpu.roll(av[0], ROWS - 1, 1))
+        low = high = jnp.zeros((64, ROWS), F32)
         for level in range(NEAR - 1):
             w = 2 ** (level + 1)
             low = jnp.where(wide >= w, pltpu.roll(cf[level, which], w, 1), low)
@@ -212,11 +219,9 @@
     for side in range(2):
         for which in range(2):
             pack = got_packs[side, which]
-            near_a[side, 1 + which] = pack
             for level in range(NEAR - 1):
                 w = 2 ** (level + 1)
-                near_c[side, level, which] = pltpu.roll(pack, w if side == 0 else ROWS - w, 1)
-        near_a[side, 0] = pltpu.roll(got_packs[side, 0], 1 if side == 0 else ROWS - 1, 1)
+                triangle[side, level, which] = pltpu.roll(pack, w if side == 0 else ROWS - w, 1)
 
     def top_blocks():
         yield 0, 0, cf.at[11]
@@ -283,13 +288,15 @@
         send_sums(sums, j + 1)
         return hess
 
-    def body(j, hess, last=False):
-        strip = [h1[j, 0] * has_below, h1[j, 1] * has_above]
-
+    def body(j, hess):
+        first, last = j == 0, j == ITERS - 1
+        sides = triangle if first else near_c
         def join(left, right, k):
+            if not first:
+                return left, right
             return (
-                jnp.where(lane >= ROWS - k, left, pltpu.roll(strip[0], k, 1)),
-                jnp.where(lane < k, right, pltpu.roll(strip[1], ROWS - k, 1)),
+                jnp.where(lane >= ROWS - k, left, pltpu.roll(xs[0, 0], k, 1)),
+                jnp.where(lane < k, right, pltpu.roll(xs[0, 2], ROWS - k, 1)),
             )
 
         left, right = join(xs[j, 0], xs[j, 2], 1)
@@ -299,10 +306,10 @@
             mid = step(cf.at[level], u[1], down(u[1], u[0], s), upward(u[1], u[2], s))
             if level < NEAR - 1:
                 left = step(
-                    near_c.at[0, level], u[0], down(u[0], u[0], s), upward(u[0], u[1], s)
+                    sides.at[0, level], u[0], down(u[0], u[0], s), upward(u[0], u[1], s)
                 ) * has_below
                 right = step(
-                    near_c.at[1, level], u[2], down(u[2], u[1], s), upward(u[2], u[2], s)
+                    sides.at[1, level], u[2], down(u[2], u[1], s), upward(u[2], u[2], s)
                 ) * has_above
                 if level < NEAR - 2:
                     left, right = join(left, right, 2 * s)
@@ -327,22 +334,17 @@
             return far_level(cf.at[level + 1], y[0], y[-2], y[2], 0, 2 * by)
 
         def after_first():
-            if not last:
-
-                @pl.when(j == 0)
-                def _():
-                    send_low(False)
-                    send_top()
-                    drain(c7, mrecv.at[1])
+            if first:
+                send_low(False)
+                send_top()
+                drain(c7, mrecv.at[1])
 
         def after_second():
-            if not last:
-
-                @pl.when(j == 0)
-                def _():
-                    drain(c9, mrecv.at[2])
-
-                pl.when(j == 1)(take_edges)
+            if first:
+                pass
+                drain(c9, mrecv.at[2])
+            elif not last:
+                take_edges()
 
         x = group(x, src2, h2, 1, c7, 7, 1, after_first)
         x = group(x, src3, h3, 2, c9, 9, 4, after_second)
@@ -356,13 +358,12 @@
             send(srct.at[j], got.at[k], rsend.at[j, 3], rrecv.at[j, 3], dev(-16 * o - c))
         pass_sums(j)
 
-        if not last:
-
-            @pl.when(j == 0)
-            def _():
-                drain(c11, mrecv.at[3])
-                drain(c12, mrecv.at[4])
-                drain(c13, mrecv.at[5])
+        if first:
+            send_operator()
+            send_near()
+            drain(c11, mrecv.at[3])
+            drain(c12, mrecv.at[4])
+            drain(c13, mrecv.at[5])
 
         drain(got, rrecv.at[j, 3])
         f = [x] + [got[o] for o in range(15)]
@@ -377,6 +378,13 @@
         y3 = {p: top(cf.at[13] if p == 0 else c13, y2, p, 4) for p in (0, 8)}
         x = top(cf.at[14], y3, 0, 8)
         x = x + mul(fv, x)
+
+        if not last:
+            src1[j + 1, 0] = x
+            src1[j + 1, 1] = x
+            ship_strips(j + 1)
+            if first:
+                send_edges()
 
         h, inverse, new, hess = finish(j, xs[j, 1], hess)
         bs[j] = new
@@ -395,9 +403,9 @@
             xs[j + 1, 1] = operate(av, 1, x, down(x, left, 1), upward(x, right, 1))
             return finish_sums(j, new, hess)
 
-        make_strips(j + 1, x, operate(av, 1, x, pltpu.roll(x, 1, 1), pltpu.roll(x, ROWS - 1, 1)))
-        ship_strips(j + 1)
-        pl.when(j == 0)(send_edges)
+        if first:
+            drain(near_a, mrecv.at[8])
+            drain(near_c, mrecv.at[7])
         drain(h1.at[j + 1], rrecv.at[j + 1, 0])
         left, right = h1[j + 1, 0] * has_below, h1[j + 1, 1] * has_above
         middle = operate(av, 1, x, down(x, left, 1), upward(x, right, 1))
@@ -409,8 +417,9 @@
 
         return finish_sums(j, new, hess)
 
-    hess = lax.fori_loop(0, ITERS - 1, body, zero)
-    hess = body(ITERS - 1, hess, True)
+    hess = zero
+    for j in range(ITERS):
+        hess = body(j, hess)
     pass_sums(ITERS)
     _, _, new, hess = finish(ITERS, xs[ITERS, 1], hess)
     basis_ref[ITERS] = new
@@ -418,6 +427,8 @@
 
     drain(packs, msend.at[0])
     drain(edges, msend.at[6])
+    drain(near_c, msend.at[7])
+    drain(near_a, msend.at[8])
     drain(c7, msend.at[1])
     drain(c9, msend.at[2])
     drain(c11, msend.at[3])
@@ -452,7 +463,8 @@
         out_specs=(pl.BlockSpec(memory_space=pltpu.VMEM), pl.BlockSpec(memory_space=pltpu.VMEM)),
         scratch_shapes=[
             vmem(*tile), vmem(3, *block), vmem(*block), vmem(15, 2, *block),
-            vmem(2, 2, *block), vmem(2, 2, *block), vmem(2, 6, 2, *block), vmem(2, 3, *block), vmem(2, 2, *block), vmem(2, 2, *block),
+            vmem(2, 2, *block), vmem(2, 2, *block), vmem(2, 6, 2, *block),
+            vmem(2, 6, 2, *block), vmem(2, 3, *block), vmem(2, 2, *block), vmem(2, 2, *block),
             vmem(7, 2, *block), vmem(3, 2, *block), vmem(2, *block),
             vmem(2, *block), vmem(2, *block), vmem(2, 4, 2, *block), vmem(2, *block),
             vmem(4, 3, *tile), vmem(4, *tile), vmem(3, *tile),
@@ -460,9 +472,9 @@
             vmem(4, 1, ROWS), vmem(4, 1, ROWS),
             vmem(3, 2, *tile), vmem(3, 6, *tile), vmem(3, 6, *tile), vmem(2, 15, *tile), vmem(47, *tile),
             vmem(4, 16, ROWS), vmem(4, 16, ROWS),
-            pltpu.SemaphoreType.DMA((7,)),
-            pltpu.SemaphoreType.DMA((7,)),
-            pltpu.SemaphoreType.DMA((7,)),
+            pltpu.SemaphoreType.DMA((9,)),
+            pltpu.SemaphoreType.DMA((9,)),
+            pltpu.SemaphoreType.DMA((9,)),
             pltpu.SemaphoreType.DMA((4, 6)),
             pltpu.SemaphoreType.DMA((4, 6)),
         ],

time: 90.9 us -> 90.2 us (level)
  no operation moved by 1% of the time
where the time goes in v7:
time: 90.2 us; the launch traced here: 90 us
  Pallas kernels  89.4 us (99%)
    pallas_call x1, Pallas kernels, on_device(): pl.pallas_call(kernel, out_shape=(jax.ShapeDtypeStruct((ITERS + 1, 8, ROW...  88.1 us

profile of v7, /device:TPU:1, one launch (start us, length us, event | category | flops | bytes accessed | tf_op | source)
XLA Modules:
  0.0 90.0 jit_solution(17675680363511121103)
XLA Ops:
  0.6 88.1 %shard_map.86 = (f32[4,8,128]{2,1,0:T(8,128)}, f32[8,128]{1,0:T(8,128)}) custom-call(f32[8,128]{1,0:T(8,128)} %r_hbm.1, f32[64,128]{1,0:T(8,128)} %bitcast.8, f32[64,128]{1,0:T(8,128)} %bitcast.9, f32[64,128]{1,0:T(8,128)} %bitcast.10, f32[15,64,128]{2,1,0:T(8,128)} %bitcast.6, f32[15,64,128]{2,1,0:T(8,128)} %bitcast.7, f32[64,128]{1,0:T(8,128)} %bitcast.11), custom_call_target="tpu_custom_call" | custom-call | tf_op jit(solution)/shard_map/pallas_call | solution.py:456
  88.7 1.3 %shard_map.87 = (f32[4,8,128]{2,1,0:T(8,128)}, f32[4,3]{1,0:T(4,128)}) custom-call(f32[4,8,128]{2,1,0:T(8,128)} %get-tuple-element.4.basis_ref, f32[8,128]{1,0:T(8,128)} %get-tuple-element.5.hess_ref), custom_call_target="tpu_custom_call" | custom-call | tf_op jit(solution)/shard_map/pallas_call | solution.py:491
